TPU v7x, 16 devices: a whole 2x2x2 slice. The times are simulated.
16 devices in a mesh: rep: 1, dp: 16 (over x, y, z, core).
Axes of the slice: x: 2, y: 2, z: 2, core: 2. Of those that a mesh axis runs over, the one named last changes fastest.
Arguments:
- g_w_gate: bfloat16 [16, 2, 1024, 4096], P(('rep', 'dp'))
- g_w_up: bfloat16 [16, 2, 1024, 4096], P(('rep', 'dp'))
- g_w_down: bfloat16 [16, 2, 4096, 1024], P(('rep', 'dp'))
- w_gate: bfloat16 [2, 1024, 4096], replicated
- w_up: bfloat16 [2, 1024, 4096], replicated
- w_down: bfloat16 [2, 4096, 1024], replicated
- m_w_gate: float32 [2, 1024, 4096], P(None, 'dp')
- m_w_up: float32 [2, 1024, 4096], P(None, 'dp')
- m_w_down: float32 [2, 4096, 1024], P(None, 'dp')
- v_w_gate: float32 [2, 1024, 4096], P(None, 'dp')
- v_w_up: float32 [2, 1024, 4096], P(None, 'dp')
- v_w_down: float32 [2, 4096, 1024], P(None, 'dp')
Outputs:
- output 1: bfloat16 [2, 1024, 4096], P('rep')
- output 2: bfloat16 [2, 1024, 4096], P('rep')
- output 3: bfloat16 [2, 4096, 1024], P('rep')
- output 4: float32 [2, 1024, 4096], P('rep', 'dp')
- output 5: float32 [2, 1024, 4096], P('rep', 'dp')
- output 6: float32 [2, 4096, 1024], P('rep', 'dp')
- output 7: float32 [2, 1024, 4096], P('rep', 'dp')
- output 8: float32 [2, 1024, 4096], P('rep', 'dp')
- output 9: float32 [2, 4096, 1024], P('rep', 'dp')
All inputs are finite; a program needn't handle non-finite values.
Results may differ from a plain program's by a relative error of at most 0.022.
Values are sent between devices in bfloat16 or wider.
A program may use at most 2 GiB of HBM per device.

v0:
```python
import jax
import jax.numpy as jnp
from jax import lax
from jax.sharding import PartitionSpec as P


def adamw(w, m, v, g):
    m = 0.9 * m + 0.1 * g
    v = 0.95 * v + 0.05 * g * g
    step = m * lax.rsqrt(v + 1e-8) + 0.1 * w
    return (w - 0.02 * step).astype(jnp.bfloat16), m, v


def clipped(gradients, sum_of_squares, count):
    factor = jnp.minimum(1.0, 0.5 * lax.rsqrt(sum_of_squares / count + 1e-30))
    return [g * factor for g in gradients]


def solution(mesh):
    def step(*arrays):
        terms, weights, m, v = (arrays[i : i + 3] for i in (0, 3, 6, 9))
        gradients = [lax.psum_scatter(t[0], "dp", scatter_dimension=1, tiled=True).astype(jnp.float32) for t in terms]
        squares = lax.psum(sum(jnp.sum(g * g) for g in gradients), "dp")
        gradients = clipped(gradients, squares, lax.psum(1, "dp") * sum(g.size for g in gradients))
        me = lax.axis_index("dp")
        own = [lax.dynamic_slice_in_dim(w, me * one.shape[1], one.shape[1], 1).astype(jnp.float32) for w, one in zip(weights, m, strict=True)]
        new = [adamw(w, m, v, g) for w, m, v, g in zip(own, m, v, gradients, strict=True)]
        whole = [lax.all_gather(one[0], "dp", axis=1, tiled=True) for one in new]
        return (*whole, *(one[1] for one in new), *(one[2] for one in new))

    all_of, cut = P(None, None, None), P(None, "dp", None)
    return jax.shard_map(
        step,
        mesh=mesh,
        in_specs=(P(("rep", "dp"), None, None, None),) * 3 + (all_of,) * 3 + (cut,) * 6,
        out_specs=(P("rep", None, None),) * 3 + (P("rep", "dp", None),) * 6,
        check_vma=False,
    )
```

profile of v0, /device:TPU:0, one launch (start us, length us, event | category | flops | bytes accessed | tf_op | source)
XLA Modules:
  0.0 862.3 jit_solution(2847279106513255836)
XLA Ops:
  7.2 0.7 reduce-scatter.4.cloned.1.call-update
  8.0 0.7 reduce-scatter.6.cloned.1.call-update
  8.7 0.7 reduce-scatter.8.cloned.1.call-update
  9.4 0.0 all-gather.8.cloned.1.call-start
  9.5 175.7 %reduce-scatter.4.cloned.1.call-done = bf16[2,64,4096]{2,1,0:T(8,128)(2,1)} async-done(((bf16[2,1024,4096]{2,1,0:T(8,128)(2,1)}), bf16[2,64,4096]{2,1,0:T(8,128)(2,1)}) %reduce-scatter.4.cloned.1.call-update) | async-done | bytes 1048592 | tf_op jit(solution)/shard_map/reduce_scatter | solution.py:22
  185.2 2.4 fusion.9
  187.5 176.0 %reduce-scatter.6.cloned.1.call-done = bf16[2,64,4096]{2,1,0:T(8,128)(2,1)} async-done(((bf16[2,1024,4096]{2,1,0:T(8,128)(2,1)}), bf16[2,64,4096]{2,1,0:T(8,128)(2,1)}) %reduce-scatter.6.cloned.1.call-update) | async-done | bytes 1048592 | tf_op jit(solution)/shard_map/reduce_scatter | solution.py:22
  363.5 2.4 fusion.10
  367.2 174.7 %reduce-scatter.8.cloned.1.call-done = bf16[2,256,1024]{2,1,0:T(8,128)(2,1)} async-done(((bf16[2,4096,1024]{2,1,0:T(8,128)(2,1)}), bf16[2,256,1024]{2,1,0:T(8,128)(2,1)}) %reduce-scatter.8.cloned.1.call-update) | async-done | bytes 1048592 | tf_op jit(solution)/shard_map/reduce_scatter | solution.py:22
  541.9 2.4 fusion.11
  544.9 35.9 %psum.7 = f32[]{:T(128)} all-reduce(f32[]{:T(128)S(6)} %add.65), channel_id=1, replica_groups=mesh['rep'=1,'dp'=16] {'dp'}, use_global_device_ids=true, to_apply=%region_6.0 | all-reduce | flops 1 | bytes 8 | tf_op jit(solution)/shard_map/psum | solution.py:23
  581.5 5.3 fusion.17
  586.9 0.0 all-gather.4.cloned.1.call-start
  586.9 5.6 fusion.8
  592.5 0.0 all-gather.6.cloned.1.call-start
  592.6 5.5 fusion.14
  598.1 65.7 %all-gather.8.cloned.1.call-done = bf16[2,4096,1024]{2,1,0:T(8,128)(2,1)} async-done(((bf16[2,256,1024]{2,1,0:T(8,128)(2,1)}), bf16[2,4096,1024]{2,1,0:T(8,128)(2,1)}) %all-gather.8.cloned.1.call-update) | async-done | bytes 16777232 | tf_op jit(solution)/shard_map/all_gather | solution.py:28
  663.9 78.7 %all-gather.4.cloned.1.call-done = bf16[2,1024,4096]{2,1,0:T(8,128)(2,1)} async-done(((bf16[2,64,4096]{2,1,0:T(8,128)(2,1)}), bf16[2,1024,4096]{2,1,0:T(8,128)(2,1)}) %all-gather.4.cloned.1.call-update) | async-done | bytes 16777232 | tf_op jit(solution)/shard_map/all_gather | solution.py:28
  742.6 78.8 %all-gather.6.cloned.1.call-done = bf16[2,1024,4096]{2,1,0:T(8,128)(2,1)} async-done(((bf16[2,64,4096]{2,1,0:T(8,128)(2,1)}), bf16[2,1024,4096]{2,1,0:T(8,128)(2,1)}) %all-gather.6.cloned.1.call-update) | async-done | bytes 16777232 | tf_op jit(solution)/shard_map/all_gather | solution.py:28
  821.4 16.8 %copy.24 = bf16[2,1024,4096]{2,1,0:T(8,128)(2,1)} copy(bf16[2,1024,4096]{2,1,0:T(8,128)(2,1)} %all-gather.4.cloned.1.call-done) | data formatting | bytes 33554432
  838.2 8.5 copy.25
  846.7 1.2 slice-done.2
  847.9 1.4 slice-done.3
  849.3 6.2 copy.26
  (21 shorter events, 0.2 us)
Async XLA Ops:
  7.2 178.0 %reduce-scatter.4.cloned.1.call-start = ((), (), s32[]{:S(2)}) async-start(), calls=%async_computation.3 | async-start | bytes 17825792 | tf_op jit(solution)/shard_map/reduce_scatter | solution.py:22
  7.9 355.6 %reduce-scatter.6.cloned.1.call-start = ((), (), s32[]{:S(2)}) async-start(), calls=%async_computation.4 | async-start | bytes 17825792 | tf_op jit(solution)/shard_map/reduce_scatter | solution.py:22
  8.7 533.2 %reduce-scatter.8.cloned.1.call-start = ((), (), s32[]{:S(2)}) async-start(), calls=%async_computation.5 | async-start | bytes 17825792 | tf_op jit(solution)/shard_map/reduce_scatter | solution.py:22
  9.4 572.1 %copy-start.3 = (f32[2,256,1024]{2,1,0:T(8,128)S(1)}, f32[2,256,1024]{2,1,0:T(8,128)}, u32[]{:S(2)}) copy-start(f32[2,256,1024]{2,1,0:T(8,128)} %param.23) | copy-start | bytes 6291460
  9.4 654.5 %all-gather.8.cloned.1.call-start = ((), (), s32[]{:S(2)}) async-start(), calls=%async_computation.8 | async-start | bytes 17825792 | tf_op jit(solution)/shard_map/all_gather | solution.py:28
  581.5 5.4 copy-start.2
  586.9 155.7 %all-gather.4.cloned.1.call-start = ((), (), s32[]{:S(2)}) async-start(), calls=%async_computation.6 | async-start | bytes 17825792 | tf_op jit(solution)/shard_map/all_gather | solution.py:28
  586.9 5.7 copy-start.1
  592.5 228.8 %all-gather.6.cloned.1.call-start = ((), (), s32[]{:S(2)}) async-start(), calls=%async_computation.7 | async-start | bytes 17825792 | tf_op jit(solution)/shard_map/all_gather | solution.py:28
  821.4 16.8 %copy-start = (bf16[2,1024,4096]{2,1,0:T(8,128)(2,1)S(1)}, bf16[2,1024,4096]{2,1,0:T(8,128)(2,1)}, u32[]{:S(2)}) copy-start(bf16[2,1024,4096]{2,1,0:T(8,128)(2,1)} %all-gather.6.cloned.1.call-done) | copy-start | bytes 50331652
  821.4 25.3 %slice-start = ((s8[16777216]{0:T(1024)(128)(4,1)}), s8[4194304]{0:T(1024)(128)(4,1)S(1)}, s32[]{:S(2)}) async-start(s8[16777216]{0:T(1024)(128)(4,1)} %bitcast.6), calls=%async_computation.9 | async-start | bytes 8388608
  821.4 25.3 %slice-start.1 = ((s8[16777216]{0:T(1024)(128)(4,1)}), s8[4194304]{0:T(1024)(128)(4,1)S(1)}, s32[]{:S(2)}) async-start(s8[16777216]{0:T(1024)(128)(4,1)} %bitcast.6), calls=%async_computation.10 | async-start | bytes 8388608
  821.4 26.5 %slice-start.2 = ((s8[16777216]{0:T(1024)(128)(4,1)}), s8[4194304]{0:T(1024)(128)(4,1)S(1)}, s32[]{:S(2)}) async-start(s8[16777216]{0:T(1024)(128)(4,1)} %bitcast.6), calls=%async_computation.11 | async-start | bytes 8388608
  838.2 11.1 %slice-start.3 = ((s8[16777216]{0:T(1024)(128)(4,1)}), s8[4194304]{0:T(1024)(128)(4,1)S(1)}, s32[]{:S(2)}) async-start(s8[16777216]{0:T(1024)(128)(4,1)} %bitcast.6), calls=%async_computation.12 | async-start | bytes 8388608
Sparse Core Ops, SparseCore 0:
  10.3 174.8 reduce-scatter.3
  187.4 176.0 reduce-scatter.5
  365.8 176.0 reduce-scatter.7
  587.0 76.8 all-gather.7
  666.6 76.0 all-gather.3
  745.3 76.0 all-gather.5
where the time goes:
time: 863 us; the launch traced here: 862 us
  waiting for transfers between devices  752 us (87%)
  blocking collectives  35.9 us (4%)
  local copies, waits for them, and re-layouts  34.1 us (4%)
  other arithmetic  23.6 us (3%)
  between operations  16.8 us (2%)
    reduce_scatter x3, waiting for transfers between devices, step(): lax.psum_scatter(t[0], 'dp', scatter_dimension=1, tiled=True)  526 us
    all_gather x3, waiting for transfers between devices, step(): whole = [lax.all_gather(one[0], 'dp', axis=1, tiled=True) for one in new]  223 us
    psum x1, blocking collectives, step(): squares = lax.psum(sum((jnp.sum(g * g) for g in gradients)), 'dp')  35.9 us
    unnamed x19, local copies, waits for them, and re-layouts  34.1 us
  transfers between devices with their start and end apart: 6, of which 6 were waited for; matrix products, arithmetic and copies ran while one was open for 2% of the time, Pallas kernels for 0%

commit v1 on v0

v1 whole, which is shorter than its diff:
```python
import functools

import jax
import jax.numpy as jnp
from jax import lax
from jax.experimental import pallas as pl
from jax.experimental.pallas import tpu as pltpu
from jax.sharding import PartitionSpec as P

MESH = pl.DeviceIdType.MESH
BF16, F32 = jnp.bfloat16, jnp.float32
DEVICES = 16
LAYERS = 2
CHUNKS = 4
JOBS = LAYERS * CHUNKS
ORDERS = ("xyz", "yzx", "zxy")
STEP = {"x": 8, "y": 4, "z": 2, "c": 1}


def adamw(w, m, v, g):
    m = 0.9 * m + 0.1 * g
    v = 0.95 * v + 0.05 * g * g
    step = m * lax.rsqrt(v + 1e-8) + 0.1 * w
    return (w - 0.02 * step).astype(jnp.bfloat16), m, v


def place(me):
    bit = {a: (me // s) % 2 for a, s in STEP.items()}
    peer = {a: me + s - 2 * s * bit[a] for a, s in STEP.items()}
    return bit, peer


def greet(me):
    barrier = pltpu.get_barrier_semaphore()
    for i in range(1, DEVICES):
        pl.semaphore_signal(barrier, inc=1, device_id={"dp": (me + i) % DEVICES}, device_id_type=MESH)
    pl.semaphore_wait(barrier, DEVICES - 1)


def send(src, dst, sems, to):
    return pltpu.make_async_remote_copy(src, dst, sems[0], sems[1], device_id={"dp": to}, device_id_type=MESH)


def at_axis(ref, lead, axes, axis, bit):
    where = tuple(bit if a == axis else slice(None) for a in axes)
    return ref.at[(*lead, *where)]


def scatter_kernel(*refs):
    g, refs = refs[:3], refs[3:]
    out, total, refs = refs[:3], refs[3], refs[4:]
    own, s0, r1, r2, r3, gb, acc = (refs[3 * i : 3 * i + 3] for i in range(7))
    mine, all_sq, own_sem, out_sem, tx, rx, sq_tx, sq_rx = refs[21:]
    me = lax.axis_index("dp")
    bit, peer = place(me)
    shapes = [r.shape[-2:] for r in r3]

    def rows(k, j):
        h = shapes[k][0]
        return j // CHUNKS, pl.ds((j % CHUNKS) * h, h)

    def own_copy(k, j):
        layer, part = rows(k, j)
        return pltpu.make_async_copy(g[k].at[layer, :, :, :, bit["c"], part], own[k].at[j % 3], own_sem.at[k, j])

    def hop(k, stage, j):
        sems = (tx.at[stage, k, j], rx.at[stage, k, j])
        a1, a2, a3 = ORDERS[k]
        if stage == 0:
            layer, part = rows(k, j)
            return send(g[k].at[layer, :, :, :, 1 - bit["c"], part], s0[k].at[j], sems, peer["c"])
        if stage == 1:
            return send(at_axis(s0[k], (j,), "xyz", a1, 1 - bit[a1]), r1[k].at[j], sems, peer[a1])
        if stage == 2:
            rest = [a for a in "xyz" if a != a1]
            return send(at_axis(r1[k], (j,), rest, a2, 1 - bit[a2]), r2[k].at[j], sems, peer[a2])
        return send(r2[k].at[j, 1 - bit[a3]], r3[k].at[j], sems, peer[a3])

    def plus(a, b):
        return (a.astype(F32) + b.astype(F32)).astype(BF16)

    def out_copy(k, j):
        layer, part = rows(k, j)
        return pltpu.make_async_copy(gb[k].at[layer, part], out[k].at[layer, part], out_sem.at[k, j])

    greet(me)
    for k in range(3):
        acc[k][...] = jnp.zeros_like(acc[k])
        for j in range(2):
            own_copy(k, j).start()
            hop(k, 0, j).start()

    def turn(s, _):
        @pl.when(s < JOBS - 2)
        def _():
            for k in range(3):
                own_copy(k, s + 2).start()
                hop(k, 0, s + 2).start()

        @pl.when(s < JOBS)
        def _():
            for k in range(3):
                own_copy(k, s).wait()
                hop(k, 0, s).wait_recv()

                @pl.loop(0, 8)
                def _(b):
                    i = (b // 4, (b // 2) % 2, b % 2)
                    s0[k][(s, *i)] = plus(own[k][(s % 3, *i)], s0[k][(s, *i)])

                hop(k, 1, s).start()

        @pl.when((s >= 1) & (s < JOBS + 1))
        def _():
            j = s - 1
            for k in range(3):
                a1 = ORDERS[k][0]
                hop(k, 1, j).wait_recv()

                @pl.loop(0, 4)
                def _(b):
                    i = [b // 2, b % 2]
                    full = list(i)
                    full.insert("xyz".index(a1), bit[a1])
                    r1[k][(j, *i)] = plus(s0[k][(j, *full)], r1[k][(j, *i)])

                hop(k, 2, j).start()

        @pl.when((s >= 2) & (s < JOBS + 2))
        def _():
            j = s - 2
            for k in range(3):
                a1, a2, _a3 = ORDERS[k]
                rest = [a for a in "xyz" if a != a1]
                hop(k, 2, j).wait_recv()

                @pl.loop(0, 2)
                def _(b):
                    full = [b]
                    full.insert(rest.index(a2), bit[a2])
                    r2[k][j, b] = plus(r1[k][(j, *full)], r2[k][j, b])

                hop(k, 3, j).start()

        @pl.when(s >= 3)
        def _():
            j = s - 3
            for k in range(3):
                a3 = ORDERS[k][2]
                hop(k, 3, j).wait_recv()
                done = plus(r2[k][j, bit[a3]], r3[k][j])
                layer, part = rows(k, j)
                gb[k][layer, part] = done
                wide = done.astype(F32)
                squares = wide * wide
                acc[k][...] += sum(squares[8 * i : 8 * i + 8] for i in range(shapes[k][0] // 8))
                out_copy(k, j).start()

        return 0

    lax.fori_loop(0, JOBS + 3, turn, 0)

    part = jnp.zeros((8, 128), F32)
    for k in range(3):
        a = acc[k][...]
        part += sum(a[:, 128 * i : 128 * i + 128] for i in range(a.shape[1] // 128))
    mine[...] = part
    all_sq[me] = part
    sends = [send(mine, all_sq.at[me], (sq_tx.at[i], sq_rx.at[i]), (me + i) % DEVICES) for i in range(1, DEVICES)]
    for one in sends:
        one.start()
    for one in sends:
        one.wait()
    total[...] = jnp.full((8, 128), jnp.sum(sum(all_sq[i] for i in range(DEVICES))), F32)

    def drain(j, _):
        for k in range(3):
            for stage in range(4):
                hop(k, stage, j).wait_send()
            out_copy(k, j).wait()
        return 0

    lax.fori_loop(0, JOBS, drain, 0)


def scatter(terms):
    blocks = [(t.shape[1] // DEVICES, t.shape[2]) for t in terms]
    split = [t.reshape(LAYERS, 2, 2, 2, 2, *b) for t, b in zip(terms, blocks, strict=True)]
    piece = [(r // CHUNKS, c) for r, c in blocks]
    sem = pltpu.SemaphoreType.DMA
    anywhere = pl.BlockSpec(memory_space=pl.ANY)
    scratch = [pltpu.VMEM((n, *lead, *p), BF16) for n, lead in ((3, (2, 2, 2)), (JOBS, (2, 2, 2)), (JOBS, (2, 2)), (JOBS, (2,)), (JOBS, ())) for p in piece]
    scratch += [pltpu.VMEM((LAYERS, *b), BF16) for b in blocks]
    scratch += [pltpu.VMEM((8, c), F32) for _, c in blocks]
    scratch += [pltpu.VMEM((8, 128), F32), pltpu.VMEM((DEVICES, 8, 128), F32)]
    scratch += [sem((3, JOBS)), sem((3, JOBS)), sem((4, 3, JOBS)), sem((4, 3, JOBS)), sem((DEVICES,)), sem((DEVICES,))]
    *sums, total = pl.pallas_call(
        scatter_kernel,
        out_shape=[jax.ShapeDtypeStruct((LAYERS, *b), BF16) for b in blocks] + [jax.ShapeDtypeStruct((8, 128), F32)],
        in_specs=[anywhere] * 3,
        out_specs=[anywhere] * 3 + [pl.BlockSpec(memory_space=pltpu.VMEM)],
        scratch_shapes=scratch,
        compiler_params=pltpu.CompilerParams(collective_id=0, has_side_effects=True, vmem_limit_bytes=62 * 2**20),
        name="scatter",
    )(*split)
    return sums, total[0, 0]


def solution(mesh):
    def step(*arrays):
        terms, weights, m, v = (arrays[i : i + 3] for i in (0, 3, 6, 9))
        sums, squares = scatter([t[0] for t in terms])
        count = DEVICES * sum(g.size for g in sums)
        factor = jnp.minimum(1.0, 0.5 * lax.rsqrt(squares / count + 1e-30))
        gradients = [g.astype(F32) * factor for g in sums]
        me = lax.axis_index("dp")
        own = [lax.dynamic_slice_in_dim(w, me * one.shape[1], one.shape[1], 1).astype(jnp.float32) for w, one in zip(weights, m, strict=True)]
        new = [adamw(w, m, v, g) for w, m, v, g in zip(own, m, v, gradients, strict=True)]
        whole = [lax.all_gather(one[0], "dp", axis=1, tiled=True) for one in new]
        return (*whole, *(one[1] for one in new), *(one[2] for one in new))

    all_of, cut = P(None, None, None), P(None, "dp", None)
    return jax.shard_map(
        step,
        mesh=mesh,
        in_specs=(P(("rep", "dp"), None, None, None),) * 3 + (all_of,) * 3 + (cut,) * 6,
        out_specs=(P("rep", None, None),) * 3 + (P("rep", "dp", None),) * 6,
        check_vma=False,
    )
```

time: 863 us -> 470 us (0.54)
  waiting for transfers between devices: 752 us -> 223 us
  Pallas kernels: 0 us -> 180 us
  blocking collectives: 35.9 us -> 0 us
    reduce_scatter x3 -> x0, waiting for transfers between devices: 526 us -> none  [step(): lax.psum_scatter(t[0], 'dp', scatter_dimension=1, tiled=True)]
    pallas_call x0 -> x1, Pallas kernels: none -> 180 us  [scatter(): pl.pallas_call(scatter_kernel, out_shape=[jax.ShapeDtypeStruct((LAYERS, *...]
    psum x1 -> x0, blocking collectives: 35.9 us -> none  [step(): squares = lax.psum(sum((jnp.sum(g * g) for g in gradients)), 'dp')]
    unnamed x19 -> x17, local copies, waits for them, and re-layouts: 34.1 us -> 34.1 us
  transfers between devices with their start and end apart: 6 -> 3, of which waited for: 6 -> 3; matrix products, arithmetic and copies ran while one was open for 2% -> 2% of each run, Pallas kernels for 0% -> 0%
where the time goes in v1:
time: 470 us
  waiting for transfers between devices  223 us (47%)
  Pallas kernels  180 us (38%)
  local copies, waits for them, and re-layouts  35.3 us (8%)
  other arithmetic  16.8 us (4%)
  between operations  14.5 us (3%)
    all_gather x3, waiting for transfers between devices, step(): whole = [lax.all_gather(one[0], 'dp', axis=1, tiled=True) for one in new]  223 us
    pallas_call x1, Pallas kernels, scatter(): pl.pallas_call(scatter_kernel, out_shape=[jax.ShapeDtypeStruct((LAYERS, *...  180 us
    unnamed x17, local copies, waits for them, and re-layouts  34.1 us
    convert_element_type x3, other arithmetic, adamw(): return ((w - 0.02 * step).astype(jnp.bfloat16), m, v)  16.8 us
  transfers between devices with their start and end apart: 3, of which 3 were waited for; matrix products, arithmetic and copies ran while one was open for 2% of the time, Pallas kernels for 0%

profile of v1, /device:TPU:0, one launch (start us, length us, event | category | flops | bytes accessed | tf_op | source)
XLA Modules:
  0.0 469.7 jit_solution(12742948466713012913)
XLA Ops:
  7.2 0.0 all-gather.4.cloned.1.call-start
  7.2 180.0 %scatter.1 = (bf16[2,64,4096]{2,1,0:T(8,128)(2,1)}, bf16[2,64,4096]{2,1,0:T(8,128)(2,1)}, bf16[2,256,1024]{2,1,0:T(8,128)(2,1)}, f32[8,128]{1,0:T(8,128)}) custom-call(bf16[2,2,2,2,2,64,4096]{6,5,4,3,2,1,0:T(8,128)(2,1)} %bitcast.4, bf16[2,2,2,2,2,64,4096]{6,5,4,3,2,1,0:T(8,128)(2,1)} %bitcast.5, bf16[2,2,2,2,2,256,1024]{6,5,4,3,2,1,0:T(8,128)(2,1)} %bitcast.6), custom_call_target="tpu_custom_call" | custom-call | tf_op jit(solution)/shard_map/scatter/pallas_call | solution.py:197
  187.2 1.2 slice.3
  189.1 0.0 copy-start.1
  189.1 6.0 %fusion.2 = (bf16[2,64,4096]{2,1,0:T(8,128)(2,1)}, f32[2,64,4096]{2,1,0:T(8,128)}, f32[2,64,4096]{2,1,0:T(8,128)}) fusion(bf16[2,1024,4096]{2,1,0:T(8,128)(2,1)} %param.15, s32[]{:T(128)S(6)} %select_n.7, f32[]{:T(128)} %bitcast.3, bf16[2,64,4096]{2,1,0:T(8,128)(2,1)} %get-tuple-element.13, f32[2,64,4096]{2,1,0:T(8,128)} %param.21, f32[2,64,4096]{2,1,0:T(8,128)} %param.18), kind=kLoop, calls=%fused_computation.11 | loop fusion | flops 8912896 | bytes 11534344 | tf_op jit(solution)/shard_map/convert_element_type | solution.py:24
  195.1 0.0 all-gather.4.cloned.1.call-update
  195.1 0.0 all-gather.8.cloned.1.call-start
  195.1 0.0 copy-done.1
  195.1 0.0 copy-start.2
  195.2 5.3 %fusion.8 = (bf16[2,256,1024]{2,1,0:T(8,128)(2,1)}, f32[2,256,1024]{2,1,0:T(8,128)}, f32[2,256,1024]{2,1,0:T(8,128)}) fusion(bf16[2,4096,1024]{2,1,0:T(8,128)(2,1)} %param.17, s32[]{:T(128)S(6)} %select_n.8, f32[]{:T(128)} %bitcast.3, bf16[2,256,1024]{2,1,0:T(8,128)(2,1)} %get-tuple-element.16, f32[2,256,1024]{2,1,0:T(8,128)S(1)} %copy-done.1, ...), kind=kLoop, calls=%fused_computation.17 | loop fusion | flops 8912896 | bytes 11534344 | tf_op jit(solution)/shard_map/convert_element_type | solution.py:24
  200.5 0.0 all-gather.8.cloned.1.call-update
  200.5 0.0 all-gather.6.cloned.1.call-start
  200.6 0.0 copy-done.2
  200.6 5.5 %fusion.5 = (bf16[2,64,4096]{2,1,0:T(8,128)(2,1)}, f32[2,64,4096]{2,1,0:T(8,128)}, f32[2,64,4096]{2,1,0:T(8,128)}) fusion(bf16[2,1024,4096]{2,1,0:T(8,128)(2,1)} %param.16, s32[]{:T(128)S(6)} %select_n.7, f32[]{:T(128)} %bitcast.3, bf16[2,64,4096]{2,1,0:T(8,128)(2,1)S(1)} %copy-done.2, f32[2,64,4096]{2,1,0:T(8,128)} %param.22, f32[2,64,4096]{2,1,0:T(8,128)} %param.19), kind=kLoop, calls=%fused_computation.14 | loop fusion | flops 8912896 | bytes 11534344 | tf_op jit(solution)/shard_map/convert_element_type | solution.py:24
  206.1 0.0 all-gather.6.cloned.1.call-update
  206.1 65.1 %all-gather.4.cloned.1.call-done = bf16[2,1024,4096]{2,1,0:T(8,128)(2,1)} async-done(((bf16[2,64,4096]{2,1,0:T(8,128)(2,1)}), bf16[2,1024,4096]{2,1,0:T(8,128)(2,1)}) %all-gather.4.cloned.1.call-update) | async-done | bytes 16777232 | tf_op jit(solution)/shard_map/all_gather | solution.py:219
  271.2 78.9 %all-gather.8.cloned.1.call-done = bf16[2,4096,1024]{2,1,0:T(8,128)(2,1)} async-done(((bf16[2,256,1024]{2,1,0:T(8,128)(2,1)}), bf16[2,4096,1024]{2,1,0:T(8,128)(2,1)}) %all-gather.8.cloned.1.call-update) | async-done | bytes 16777232 | tf_op jit(solution)/shard_map/all_gather | solution.py:219
  350.1 78.9 %all-gather.6.cloned.1.call-done = bf16[2,1024,4096]{2,1,0:T(8,128)(2,1)} async-done(((bf16[2,64,4096]{2,1,0:T(8,128)(2,1)}), bf16[2,1024,4096]{2,1,0:T(8,128)(2,1)}) %all-gather.6.cloned.1.call-update) | async-done | bytes 16777232 | tf_op jit(solution)/shard_map/all_gather | solution.py:219
  429.0 16.8 %copy.24 = bf16[2,1024,4096]{2,1,0:T(8,128)(2,1)} copy(bf16[2,1024,4096]{2,1,0:T(8,128)(2,1)} %all-gather.4.cloned.1.call-done) | data formatting | bytes 33554432
  445.8 0.0 copy-done
  445.8 8.5 %copy.25 = bf16[2,1024,4096]{2,1,0:T(8,128)(2,1)} copy(bf16[2,1024,4096]{2,1,0:T(8,128)(2,1)S(1)} %copy-done) | data formatting | bytes 33554432
  454.3 1.4 slice-done.2
  455.8 1.2 slice-done.3
  457.0 6.2 %copy.26 = bf16[2,4096,1024]{2,1,0:T(8,128)(2,1)} copy(bf16[2,4096,1024]{2,1,0:T(8,128)(2,1)S(1)} %bitcast.8) | data formatting | bytes 33554432
  (8 shorter events, 0.0 us)
Async XLA Ops:
  7.2 264.1 %all-gather.4.cloned.1.call-start = ((), (), s32[]{:S(2)}) async-start(), calls=%async_computation | async-start | bytes 17825792 | tf_op jit(solution)/shard_map/all_gather | solution.py:219
  189.1 6.1 %copy-start.1 = (f32[2,256,1024]{2,1,0:T(8,128)S(1)}, f32[2,256,1024]{2,1,0:T(8,128)}, u32[]{:S(2)}) copy-start(f32[2,256,1024]{2,1,0:T(8,128)} %param.23) | copy-start | bytes 6291460
  195.1 155.1 %all-gather.8.cloned.1.call-start = ((), (), s32[]{:S(2)}) async-start(), calls=%async_computation.2 | async-start | bytes 17825792 | tf_op jit(solution)/shard_map/all_gather | solution.py:219
  195.1 5.4 %copy-start.2 = (bf16[2,64,4096]{2,1,0:T(8,128)(2,1)S(1)}, bf16[2,64,4096]{2,1,0:T(8,128)(2,1)}, u32[]{:S(2)}) copy-start(bf16[2,64,4096]{2,1,0:T(8,128)(2,1)} %get-tuple-element.15) | copy-start | bytes 3145732
  200.5 228.5 %all-gather.6.cloned.1.call-start = ((), (), s32[]{:S(2)}) async-start(), calls=%async_computation.1 | async-start | bytes 17825792 | tf_op jit(solution)/shard_map/all_gather | solution.py:219
  429.0 16.8 %copy-start = (bf16[2,1024,4096]{2,1,0:T(8,128)(2,1)S(1)}, bf16[2,1024,4096]{2,1,0:T(8,128)(2,1)}, u32[]{:S(2)}) copy-start(bf16[2,1024,4096]{2,1,0:T(8,128)(2,1)} %all-gather.6.cloned.1.call-done) | copy-start | bytes 50331652
  429.0 25.3 %slice-start = ((s8[16777216]{0:T(1024)(128)(4,1)}), s8[4194304]{0:T(1024)(128)(4,1)S(1)}, s32[]{:S(2)}) async-start(s8[16777216]{0:T(1024)(128)(4,1)} %bitcast.7), calls=%async_computation.3 | async-start | bytes 8388608
  429.0 25.3 %slice-start.1 = ((s8[16777216]{0:T(1024)(128)(4,1)}), s8[4194304]{0:T(1024)(128)(4,1)S(1)}, s32[]{:S(2)}) async-start(s8[16777216]{0:T(1024)(128)(4,1)} %bitcast.7), calls=%async_computation.4 | async-start | bytes 8388608
  445.8 9.9 %slice-start.2 = ((s8[16777216]{0:T(1024)(128)(4,1)}), s8[4194304]{0:T(1024)(128)(4,1)S(1)}, s32[]{:S(2)}) async-start(s8[16777216]{0:T(1024)(128)(4,1)} %bitcast.7), calls=%async_computation.5 | async-start | bytes 8388608
  445.8 11.1 %slice-start.3 = ((s8[16777216]{0:T(1024)(128)(4,1)}), s8[4194304]{0:T(1024)(128)(4,1)S(1)}, s32[]{:S(2)}) async-start(s8[16777216]{0:T(1024)(128)(4,1)} %bitcast.7), calls=%async_computation.6 | async-start | bytes 8388608
Sparse Core Ops, SparseCore 0:
  195.2 75.9 all-gather.3
  274.1 76.0 all-gather.7
  353.0 76.0 all-gather.5

commit v2 on v1

--- a/solution.py
+++ b/solution.py
@@ -14,6 +14,7 @@
 CHUNKS = 4
 JOBS = LAYERS * CHUNKS
 ORDERS = ("xyz", "yzx", "zxy")
+SPACES = (pltpu.VMEM, pltpu.VMEM, pltpu.HBM)
 STEP = {"x": 8, "y": 4, "z": 2, "c": 1}
 
 
@@ -206,6 +207,93 @@
     return sums, total[0, 0]
 
 
+def gather_kernel(*refs):
+    w, refs = refs[:3], refs[3:]
+    whole, (own_sem, own_tx, own_rx, tx, rx, ftx, frx) = refs[:3], refs[3:]
+    me = lax.axis_index("dp")
+    bit, peer = place(me)
+    heights = [r.shape[-2] // CHUNKS for r in whole]
+
+    def own_copy(k):
+        return pltpu.make_async_copy(w[k], whole[k].at[:, bit["x"], bit["y"], bit["z"], bit["c"]], own_sem.at[k])
+
+    def region(k, j, bits):
+        h = heights[k]
+        where = tuple(bits.get(a, slice(None)) for a in "xyz")
+        return whole[k].at[(j // CHUNKS, *where, bit["c"], pl.ds((j % CHUNKS) * h, h))]
+
+    def hop(k, stage, j):
+        axes = ORDERS[k][: 3 - stage]
+        part = region(k, j, {a: bit[a] for a in axes})
+        return send(part, part, (tx.at[stage, k, j], rx.at[stage, k, j]), peer[ORDERS[k][2 - stage]])
+
+    def forward(k, stage, j):
+        bits = {a: bit[a] for a in ORDERS[k][: 3 - stage]}
+        axis = ORDERS[k][2 - stage]
+        bits[axis] = 1 - bit[axis]
+        part = region(k, j, bits)
+        return send(part, part, (ftx.at[stage, k, j], frx.at[stage, k, j]), peer["c"])
+
+    def own_forward(k):
+        part = whole[k].at[:, bit["x"], bit["y"], bit["z"], bit["c"]]
+        return send(part, part, (own_tx.at[k], own_rx.at[k]), peer["c"])
+
+    for k in range(3):
+        own_copy(k).start()
+    greet(me)
+    for k in range(3):
+        own_copy(k).wait()
+
+    def first(j, _):
+        for k in range(3):
+            hop(k, 0, j).start()
+        return 0
+
+    lax.fori_loop(0, JOBS, first, 0)
+    for k in range(3):
+        own_forward(k).start()
+
+    def turn(s, _):
+        for stage in range(3):
+            @pl.when((s >= stage) & (s < JOBS + stage))
+            def _():
+                j = s - stage
+                for k in range(3):
+                    hop(k, stage, j).wait_recv()
+                    if stage < 2:
+                        hop(k, stage + 1, j).start()
+                    forward(k, stage, j).start()
+        return 0
+
+    lax.fori_loop(0, JOBS + 2, turn, 0)
+
+    def drain(j, _):
+        for k in range(3):
+            for stage in range(3):
+                hop(k, stage, j).wait_send()
+                forward(k, stage, j).wait()
+        return 0
+
+    lax.fori_loop(0, JOBS, drain, 0)
+    for k in range(3):
+        own_forward(k).wait()
+
+
+def gather(blocks):
+    shapes = [b.shape[1:] for b in blocks]
+    sem = pltpu.SemaphoreType.DMA
+    whole = pl.pallas_call(
+        gather_kernel,
+        out_shape=[space((LAYERS, 2, 2, 2, 2, *s), BF16) for s, space in zip(shapes, SPACES, strict=True)],
+        in_specs=[pl.BlockSpec(memory_space=pltpu.HBM)] * 3,
+        out_specs=[pl.BlockSpec(memory_space=space) for space in SPACES],
+        scratch_shapes=[sem((3,))] * 3 + [sem((3, 3, JOBS))] * 4,
+        compiler_params=pltpu.CompilerParams(collective_id=1, has_side_effects=True, vmem_limit_bytes=2**20),
+        name="gather",
+    )(*blocks)
+    return [t.reshape(LAYERS, DEVICES * s[0], s[1]) for t, s in zip(whole, shapes, strict=True)]
+
+
 def solution(mesh):
     def step(*arrays):
         terms, weights, m, v = (arrays[i : i + 3] for i in (0, 3, 6, 9))
@@ -216,7 +304,7 @@
         me = lax.axis_index("dp")
         own = [lax.dynamic_slice_in_dim(w, me * one.shape[1], one.shape[1], 1).astype(jnp.float32) for w, one in zip(weights, m, strict=True)]
         new = [adamw(w, m, v, g) for w, m, v, g in zip(own, m, v, gradients, strict=True)]
-        whole = [lax.all_gather(one[0], "dp", axis=1, tiled=True) for one in new]
+        whole = gather([one[0] for one in new])
         return (*whole, *(one[1] for one in new), *(one[2] for one in new))
 
     all_of, cut = P(None, None, None), P(None, "dp", None)

time: 470 us -> 387 us (0.82)
  waiting for transfers between devices: 223 us -> 0 us
  Pallas kernels: 180 us -> 347 us
  between operations: 14.5 us -> 1.45 us
  local copies, waits for them, and re-layouts: 35.3 us -> 26.3 us
  other arithmetic: 16.8 us -> 11.8 us
    all_gather x3 -> x0, waiting for transfers between devices: 223 us -> none  [step(): whole = [lax.all_gather(one[0], 'dp', axis=1, tiled=True) for one in new]]
    pallas_call x0 -> x1, Pallas kernels: none -> 167 us  [gather(): pl.pallas_call(gather_kernel, out_shape=[space((LAYERS, 2, 2, 2, 2, *s),...]
    unnamed x17 -> x23, local copies, waits for them, and re-layouts: 34.1 us -> 25.1 us
    convert_element_type x3 -> x2, other arithmetic: 16.8 us -> 11.8 us  [adamw(): return ((w - 0.02 * step).astype(jnp.bfloat16), m, v)]
  transfers between devices with their start and end apart: 3 -> 0, of which waited for: 3 -> 0; matrix products, arithmetic and copies ran while one was open for 2% -> 0% of each run, Pallas kernels for 0% -> 0%
where the time goes in v2:
time: 387 us
  Pallas kernels  347 us (90%)
  local copies, waits for them, and re-layouts  26.3 us (7%)
  other arithmetic  11.8 us (3%)
    pallas_call x1, Pallas kernels, scatter(): pl.pallas_call(scatter_kernel, out_shape=[jax.ShapeDtypeStruct((LAYERS, *...  180 us
    pallas_call x1, Pallas kernels, gather(): pl.pallas_call(gather_kernel, out_shape=[space((LAYERS, 2, 2, 2, 2, *s),...  167 us
    unnamed x23, local copies, waits for them, and re-layouts  25.1 us
    convert_element_type x2, other arithmetic, adamw(): return ((w - 0.02 * step).astype(jnp.bfloat16), m, v)  11.8 us

profile of v2, /device:TPU:0, one launch (start us, length us, event | category | flops | bytes accessed | tf_op | source)
XLA Modules:
  0.0 386.6 jit_solution(11893329302626259202)
XLA Ops:
  0.6 180.0 %scatter.1 = (bf16[2,64,4096]{2,1,0:T(8,128)(2,1)}, bf16[2,64,4096]{2,1,0:T(8,128)(2,1)}, bf16[2,256,1024]{2,1,0:T(8,128)(2,1)}, f32[8,128]{1,0:T(8,128)}) custom-call(bf16[2,2,2,2,2,64,4096]{6,5,4,3,2,1,0:T(8,128)(2,1)} %bitcast.9, bf16[2,2,2,2,2,64,4096]{6,5,4,3,2,1,0:T(8,128)(2,1)} %bitcast.10, bf16[2,2,2,2,2,256,1024]{6,5,4,3,2,1,0:T(8,128)(2,1)} %bitcast.11), custom_call_target="tpu_custom_call" | custom-call | tf_op jit(solution)/shard_map/scatter/pallas_call | solution.py:198
  180.6 1.2 slice.3
  182.5 0.0 copy-start
  182.5 0.0 copy-start.1
  182.5 0.0 copy-start.2
  182.5 0.0 copy-start.3
  182.6 0.0 copy-start.4
  182.6 0.0 copy-start.5
  182.6 6.4 %fusion.8 = (bf16[2,256,1024]{2,1,0:T(8,128)(2,1)S(1)}, f32[2,256,1024]{2,1,0:T(8,128)}, f32[2,256,1024]{2,1,0:T(8,128)}) fusion(bf16[2,4096,1024]{2,1,0:T(8,128)(2,1)} %param.17, s32[]{:T(128)S(6)} %select_n.8, f32[]{:T(128)} %bitcast.3, bf16[2,256,1024]{2,1,0:T(8,128)(2,1)} %get-tuple-element.19, f32[2,256,1024]{2,1,0:T(8,128)} %param.23, ...), kind=kLoop, calls=%fused_computation.17 | loop fusion | flops 8912896 | bytes 11534344 | tf_op jit(solution)/shard_map/convert_element_type | solution.py:25
  189.0 0.0 copy-done
  189.0 0.0 copy-done.1
  189.0 0.0 copy-done.2
  189.0 0.0 copy-done.3
  189.0 0.0 copy-done.4
  189.0 0.8 copy-done.5
  189.8 5.4 %fusion.2 = (bf16[2,64,4096]{2,1,0:T(8,128)(2,1)S(1)}, f32[2,64,4096]{2,1,0:T(8,128)}, f32[2,64,4096]{2,1,0:T(8,128)}, bf16[2,64,4096]{2,1,0:T(8,128)(2,1)S(1)},...) fusion(bf16[2,1024,4096]{2,1,0:T(8,128)(2,1)} %param.15, s32[]{:T(128)S(6)} %select_n.7, f32[]{:T(128)} %bitcast.3, ...), kind=kLoop, calls=%fused_computation.11 | loop fusion | flops 17825792 | bytes 23068680 | tf_op jit(solution)/shard_map/convert_element_type | solution.py:25
  195.2 167.1 %gather.1 = (bf16[2,2,2,2,2,64,4096]{6,5,4,3,2,1,0:T(8,128)(2,1)S(1)}, bf16[2,2,2,2,2,64,4096]{6,5,4,3,2,1,0:T(8,128)(2,1)S(1)}, bf16[2,2,2,2,2,256,1024]{6,5,4,3,2,1,0:T(8,128)(2,1)}) custom-call(bf16[2,64,4096]{2,1,0:T(8,128)(2,1)S(1)} %get-tuple-element.29.refs_0_, bf16[2,64,4096]{2,1,0:T(8,128)(2,1)S(1)} %get-tuple-element.32.refs_1_, ...), custom_call_target="tpu_custom_call" | custom-call | tf_op jit(solution)/shard_map/gather/pallas_call | solution.py:285
  362.4 0.0 slice-start
  362.4 0.0 slice-start.1
  362.4 8.5 %copy.24 = bf16[2,1024,4096]{2,1,0:T(8,128)(2,1)} copy(bf16[2,1024,4096]{2,1,0:T(8,128)(2,1)S(1)} %bitcast.8) | data formatting | bytes 33554432
  370.9 8.4 %copy.25 = bf16[2,1024,4096]{2,1,0:T(8,128)(2,1)} copy(bf16[2,1024,4096]{2,1,0:T(8,128)(2,1)S(1)} %bitcast.7) | data formatting | bytes 33554432
  379.3 0.0 slice-done
  379.4 1.1 slice-done.3
  380.5 6.2 %copy.26 = bf16[2,4096,1024]{2,1,0:T(8,128)(2,1)} copy(bf16[2,4096,1024]{2,1,0:T(8,128)(2,1)S(1)} %bitcast.14) | data formatting | bytes 33554432
  (5 shorter events, 0.0 us)
Async XLA Ops:
  182.5 6.4 %copy-start = (f32[2,64,4096]{2,1,0:T(8,128)S(1)}, f32[2,64,4096]{2,1,0:T(8,128)}, u32[]{:S(2)}) copy-start(f32[2,64,4096]{2,1,0:T(8,128)} %param.21) | copy-start | bytes 6291460
  182.5 6.4 %copy-start.1 = (f32[2,64,4096]{2,1,0:T(8,128)S(1)}, f32[2,64,4096]{2,1,0:T(8,128)}, u32[]{:S(2)}) copy-start(f32[2,64,4096]{2,1,0:T(8,128)} %param.18) | copy-start | bytes 6291460
  182.5 6.4 %copy-start.2 = (f32[2,64,4096]{2,1,0:T(8,128)S(1)}, f32[2,64,4096]{2,1,0:T(8,128)}, u32[]{:S(2)}) copy-start(f32[2,64,4096]{2,1,0:T(8,128)} %param.22) | copy-start | bytes 6291460
  182.5 6.4 %copy-start.3 = (f32[2,64,4096]{2,1,0:T(8,128)S(1)}, f32[2,64,4096]{2,1,0:T(8,128)}, u32[]{:S(2)}) copy-start(f32[2,64,4096]{2,1,0:T(8,128)} %param.19) | copy-start | bytes 6291460
  182.6 6.4 %copy-start.4 = (bf16[2,64,4096]{2,1,0:T(8,128)(2,1)S(1)}, bf16[2,64,4096]{2,1,0:T(8,128)(2,1)}, u32[]{:S(2)}) copy-start(bf16[2,64,4096]{2,1,0:T(8,128)(2,1)} %get-tuple-element.16) | copy-start | bytes 3145732
  182.6 7.2 %copy-start.5 = (bf16[2,64,4096]{2,1,0:T(8,128)(2,1)S(1)}, bf16[2,64,4096]{2,1,0:T(8,128)(2,1)}, u32[]{:S(2)}) copy-start(bf16[2,64,4096]{2,1,0:T(8,128)(2,1)} %get-tuple-element.18) | copy-start | bytes 3145732
  362.4 17.0 %slice-start = ((s8[16777216]{0:T(1024)(128)(4,1)}), s8[4194304]{0:T(1024)(128)(4,1)S(1)}, s32[]{:S(2)}) async-start(s8[16777216]{0:T(1024)(128)(4,1)} %bitcast.12), calls=%async_computation | async-start | bytes 8388608
  362.4 16.9 %slice-start.1 = ((s8[16777216]{0:T(1024)(128)(4,1)}), s8[4194304]{0:T(1024)(128)(4,1)S(1)}, s32[]{:S(2)}) async-start(s8[16777216]{0:T(1024)(128)(4,1)} %bitcast.12), calls=%async_computation.1 | async-start | bytes 8388608
  370.9 8.4 %slice-start.2 = ((s8[16777216]{0:T(1024)(128)(4,1)}), s8[4194304]{0:T(1024)(128)(4,1)S(1)}, s32[]{:S(2)}) async-start(s8[16777216]{0:T(1024)(128)(4,1)} %bitcast.12), calls=%async_computation.2 | async-start | bytes 8388608
  370.9 9.5 %slice-start.3 = ((s8[16777216]{0:T(1024)(128)(4,1)}), s8[4194304]{0:T(1024)(128)(4,1)S(1)}, s32[]{:S(2)}) async-start(s8[16777216]{0:T(1024)(128)(4,1)} %bitcast.12), calls=%async_computation.3 | async-start | bytes 8388608

commit v3 on v2

v3 whole, which is shorter than its diff:
```python
import functools

import jax
import jax.numpy as jnp
from jax import lax
from jax.experimental import pallas as pl
from jax.experimental.pallas import tpu as pltpu
from jax.sharding import PartitionSpec as P

MESH = pl.DeviceIdType.MESH
BF16, F32 = jnp.bfloat16, jnp.float32
DEVICES = 16
LAYERS = 2
CUTS = ((4, 2), (4, 2), (8, 1))
CHUNKS = 8
JOBS = LAYERS * CHUNKS
SLOTS, AHEAD = 6, 2
GATHER_CHUNKS = 4
GATHER_JOBS = LAYERS * GATHER_CHUNKS
SCATTER_VMEM = 36
ORDERS = ("xyz", "yzx", "zxy")
STEP = {"x": 8, "y": 4, "z": 2, "c": 1}


def adamw(w, m, v, g):
    m = 0.9 * m + 0.1 * g
    v = 0.95 * v + 0.05 * g * g
    step = m * lax.rsqrt(v + 1e-8) + 0.1 * w
    return (w - 0.02 * step).astype(jnp.bfloat16), m, v


def place(me):
    bit = {a: (me // s) % 2 for a, s in STEP.items()}
    peer = {a: me + s - 2 * s * bit[a] for a, s in STEP.items()}
    return bit, peer


def greet(me):
    barrier = pltpu.get_barrier_semaphore()
    for i in range(1, DEVICES):
        pl.semaphore_signal(barrier, inc=1, device_id={"dp": (me + i) % DEVICES}, device_id_type=MESH)
    pl.semaphore_wait(barrier, DEVICES - 1)


def send(src, dst, sems, to):
    return pltpu.make_async_remote_copy(src, dst, sems[0], sems[1], device_id={"dp": to}, device_id_type=MESH)


def at_axis(ref, lead, axes, axis, bit):
    where = tuple(bit if a == axis else slice(None) for a in axes)
    return ref.at[(*lead, *where)]


def scatter_kernel(*refs):
    g, w, moments, refs = refs[:3], refs[3:6], refs[6:12], refs[12:]
    gb, total, own_w, held, refs = refs[:3], refs[3], refs[4:7], refs[7:13], refs[13:]
    own, s0, r1, r2, r3, acc = (refs[3 * i : 3 * i + 3] for i in range(6))
    mine, all_sq, own_sem, tx, rx, sq_tx, sq_rx, held_sem, free = refs[18:]
    me = lax.axis_index("dp")
    bit, peer = place(me)

    def piece(k, j):
        (h, w), n = r3[k].shape[-2:], CUTS[k][1]
        c = j % CHUNKS
        return j // CHUNKS, pl.ds((c // n) * h, h), pl.ds(pl.multiple_of((c % n) * w, w), w)

    def own_copy(k, j):
        layer, rows, cols = piece(k, j)
        return pltpu.make_async_copy(g[k].at[layer, :, :, :, bit["c"], rows, cols], own[k].at[j % 3], own_sem.at[k, j])

    def hop(k, stage, j):
        sems = (tx.at[stage, k, j], rx.at[stage, k, j])
        a1, a2, a3 = ORDERS[k]
        if stage == 0:
            layer, rows, cols = piece(k, j)
            return send(g[k].at[layer, :, :, :, 1 - bit["c"], rows, cols], s0[k].at[j % SLOTS], sems, peer["c"])
        if stage == 1:
            return send(at_axis(s0[k], (j % SLOTS,), "xyz", a1, 1 - bit[a1]), r1[k].at[j], sems, peer[a1])
        if stage == 2:
            rest = [a for a in "xyz" if a != a1]
            return send(at_axis(r1[k], (j,), rest, a2, 1 - bit[a2]), r2[k].at[j], sems, peer[a2])
        return send(r2[k].at[j, 1 - bit[a3]], r3[k].at[j], sems, peer[a3])

    def plus(a, b):
        return (a.astype(F32) + b.astype(F32)).astype(BF16)

    def fetch(j):
        for k in range(3):
            own_copy(k, j).start()
            hop(k, 0, j).start()

    staged = [pltpu.make_async_copy(w[k].at[:, bit["x"], bit["y"], bit["z"], bit["c"]], own_w[k], held_sem.at[k]) for k in range(3)]
    staged += [pltpu.make_async_copy(moments[i], held[i], held_sem.at[3 + i]) for i in range(6)]

    greet(me)
    for j in range(AHEAD):
        fetch(j)
    for one in staged:
        one.start()
    for k in range(3):
        acc[k][...] = jnp.zeros_like(acc[k])

    def turn(s, _):
        @pl.when((s >= SLOTS - AHEAD) & (s < JOBS - AHEAD))
        def _():
            pl.semaphore_wait(free, 1)

        @pl.when(s < JOBS - AHEAD)
        def _():
            fetch(s + AHEAD)

        @pl.when(s < JOBS)
        def _():
            for k in range(3):
                own_copy(k, s).wait()
                hop(k, 0, s).wait_recv()

                @pl.loop(0, 8)
                def _(b):
                    i = (b // 4, (b // 2) % 2, b % 2)
                    s0[k][(s % SLOTS, *i)] = plus(own[k][(s % 3, *i)], s0[k][(s % SLOTS, *i)])

                hop(k, 1, s).start()

        @pl.when((s >= 1) & (s < JOBS + 1))
        def _():
            j = s - 1
            for k in range(3):
                a1 = ORDERS[k][0]
                hop(k, 1, j).wait_recv()

                @pl.loop(0, 4)
                def _(b):
                    i = [b // 2, b % 2]
                    full = list(i)
                    full.insert("xyz".index(a1), bit[a1])
                    r1[k][(j, *i)] = plus(s0[k][(j % SLOTS, *full)], r1[k][(j, *i)])

                hop(k, 2, j).start()
            for k in range(3):
                hop(k, 1, j).wait_send()

            @pl.when(j < JOBS - SLOTS)
            def _():
                pl.semaphore_signal(free, inc=1, device_id={"dp": peer["c"]}, device_id_type=MESH)

        @pl.when((s >= 2) & (s < JOBS + 2))
        def _():
            j = s - 2
            for k in range(3):
                a1, a2, _a3 = ORDERS[k]
                rest = [a for a in "xyz" if a != a1]
                hop(k, 2, j).wait_recv()

                @pl.loop(0, 2)
                def _(b):
                    full = [b]
                    full.insert(rest.index(a2), bit[a2])
                    r2[k][j, b] = plus(r1[k][(j, *full)], r2[k][j, b])

                hop(k, 3, j).start()

        @pl.when(s >= 3)
        def _():
            j = s - 3
            for k in range(3):
                a3 = ORDERS[k][2]
                hop(k, 3, j).wait_recv()
                done = plus(r2[k][j, bit[a3]], r3[k][j])
                gb[k][piece(k, j)] = done
                wide = done.astype(F32)
                squares = wide * wide
                acc[k][...] += sum(squares[8 * i : 8 * i + 8] for i in range(done.shape[0] // 8))

        return 0

    lax.fori_loop(0, JOBS + 3, turn, 0)

    part = jnp.zeros((8, 128), F32)
    for k in range(3):
        a = acc[k][...]
        part += sum(a[:, 128 * i : 128 * i + 128] for i in range(a.shape[1] // 128))
    mine[...] = part
    all_sq[me] = part
    sends = [send(mine, all_sq.at[me], (sq_tx.at[i], sq_rx.at[i]), (me + i) % DEVICES) for i in range(1, DEVICES)]
    for one in sends:
        one.start()

    def drain(j, _):
        for k in range(3):
            for stage in (0, 2, 3):
                hop(k, stage, j).wait_send()
        return 0

    lax.fori_loop(0, JOBS, drain, 0)
    for one in staged:
        one.wait()
    for one in sends:
        one.wait()
    total[...] = jnp.full((8, 128), jnp.sum(sum(all_sq[i] for i in range(DEVICES))), F32)


def scatter(terms, weights, moments):
    blocks = [(t.shape[1] // DEVICES, t.shape[2]) for t in terms]
    split = [t.reshape(LAYERS, 2, 2, 2, 2, *b) for t, b in zip((*terms, *weights), (*blocks, *blocks), strict=True)]
    pieces = [(r // m, c // n) for (r, c), (m, n) in zip(blocks, CUTS, strict=True)]
    sem = pltpu.SemaphoreType.DMA
    leads = ((3, 2, 2, 2), (SLOTS, 2, 2, 2), (JOBS, 2, 2), (JOBS, 2), (JOBS,))
    scratch = [pltpu.VMEM((*lead, *p), BF16) for lead in leads for p in pieces]
    scratch += [pltpu.VMEM((8, c), F32) for _, c in pieces]
    scratch += [pltpu.VMEM((8, 128), F32), pltpu.VMEM((DEVICES, 8, 128), F32)]
    scratch += [sem((3, JOBS)), sem((4, 3, JOBS)), sem((4, 3, JOBS)), sem((DEVICES,)), sem((DEVICES,)), sem((9,)), pltpu.SemaphoreType.REGULAR]
    sums_0, sums_1, sums_2, total, *held = pl.pallas_call(
        scatter_kernel,
        out_shape=[pltpu.VMEM((LAYERS, *b), BF16) for b in blocks] + [pltpu.VMEM((8, 128), F32)] + [pltpu.VMEM((LAYERS, *b), BF16) for b in blocks] + [pltpu.VMEM(m.shape, F32) for m in moments],
        in_specs=[pl.BlockSpec(memory_space=pltpu.HBM)] * 12,
        out_specs=[pl.BlockSpec(memory_space=pltpu.VMEM)] * 13,
        scratch_shapes=scratch,
        compiler_params=pltpu.CompilerParams(collective_id=0, has_side_effects=True, vmem_limit_bytes=SCATTER_VMEM * 2**20),
        name="scatter",
    )(*split, *moments)
    return (sums_0, sums_1, sums_2), total[0, 0], held[:3], held[3:6], held[6:]


def gather_kernel(*refs):
    w, refs = refs[:3], refs[3:]
    whole, (own_tx, own_rx, tx, rx, ftx, frx) = refs[:3], refs[3:]
    me = lax.axis_index("dp")
    bit, peer = place(me)
    heights = [r.shape[-2] // GATHER_CHUNKS for r in whole]

    def region(k, j, bits):
        h = heights[k]
        where = tuple(bits.get(a, slice(None)) for a in "xyz")
        return whole[k].at[(j // GATHER_CHUNKS, *where, bit["c"], pl.ds((j % GATHER_CHUNKS) * h, h))]

    def hop(k, stage, j):
        axes = ORDERS[k][: 3 - stage]
        part = region(k, j, {a: bit[a] for a in axes})
        if stage == 0:
            h = heights[k]
            source = w[k].at[j // GATHER_CHUNKS, pl.ds((j % GATHER_CHUNKS) * h, h)]
        else:
            source = part
        return send(source, part, (tx.at[stage, k, j], rx.at[stage, k, j]), peer[ORDERS[k][2 - stage]])

    def forward(k, stage, j):
        bits = {a: bit[a] for a in ORDERS[k][: 3 - stage]}
        axis = ORDERS[k][2 - stage]
        bits[axis] = 1 - bit[axis]
        part = region(k, j, bits)
        return send(part, part, (ftx.at[stage, k, j], frx.at[stage, k, j]), peer["c"])

    def own_forward(k):
        part = whole[k].at[:, bit["x"], bit["y"], bit["z"], bit["c"]]
        return send(w[k], part, (own_tx.at[k], own_rx.at[k]), peer["c"])

    greet(me)

    def first(j, _):
        for k in range(3):
            hop(k, 0, j).start()
        return 0

    lax.fori_loop(0, GATHER_JOBS, first, 0)
    for k in range(3):
        own_forward(k).start()
    for k in range(3):
        whole[k][:, bit["x"], bit["y"], bit["z"], bit["c"]] = w[k][...]

    def turn(s, _):
        for stage in range(3):
            @pl.when((s >= stage) & (s < GATHER_JOBS + stage))
            def _():
                j = s - stage
                for k in range(3):
                    hop(k, stage, j).wait_recv()
                    if stage < 2:
                        hop(k, stage + 1, j).start()
                    forward(k, stage, j).start()
        return 0

    lax.fori_loop(0, GATHER_JOBS + 2, turn, 0)

    def drain(j, _):
        for k in range(3):
            for stage in range(3):
                hop(k, stage, j).wait_send()
                forward(k, stage, j).wait()
        return 0

    lax.fori_loop(0, GATHER_JOBS, drain, 0)
    for k in range(3):
        own_forward(k).wait()


def land_kernel(held, out, sem):
    one = pltpu.make_async_copy(held, out, sem)
    one.start()
    one.wait()


def gather(blocks):
    shapes = [b.shape[1:] for b in blocks]
    sem = pltpu.SemaphoreType.DMA
    whole = pl.pallas_call(
        gather_kernel,
        out_shape=[pltpu.VMEM((LAYERS, 2, 2, 2, 2, *s), BF16) for s in shapes],
        in_specs=[pl.BlockSpec(memory_space=pltpu.VMEM)] * 3,
        out_specs=[pl.BlockSpec(memory_space=pltpu.VMEM)] * 3,
        scratch_shapes=[sem((3,))] * 2 + [sem((3, 3, GATHER_JOBS))] * 4,
        compiler_params=pltpu.CompilerParams(collective_id=1, has_side_effects=True, vmem_limit_bytes=2**20),
        name="gather",
    )(*blocks)
    landed = [
        pl.pallas_call(
            land_kernel,
            out_shape=jax.ShapeDtypeStruct(t.shape, BF16),
            in_specs=[pl.BlockSpec(memory_space=pl.ANY)],
            out_specs=pl.BlockSpec(memory_space=pltpu.HBM),
            scratch_shapes=[sem],
            compiler_params=pltpu.CompilerParams(vmem_limit_bytes=2**19),
            name="land",
        )(t)
        for t in whole
    ]
    return [t.reshape(LAYERS, DEVICES * s[0], s[1]) for t, s in zip(landed, shapes, strict=True)]


def solution(mesh):
    def step(*arrays):
        terms, weights, m, v = (arrays[i : i + 3] for i in (0, 3, 6, 9))
        sums, squares, own, m, v = scatter([t[0] for t in terms], weights, (*m, *v))
        count = DEVICES * sum(g.size for g in sums)
        factor = jnp.minimum(1.0, 0.5 * lax.rsqrt(squares / count + 1e-30))
        gradients = [g.astype(F32) * factor for g in sums]
        new = [adamw(w.astype(F32), m, v, g) for w, m, v, g in zip(own, m, v, gradients, strict=True)]
        whole = gather([one[0] for one in new])
        return (*whole, *(one[1] for one in new), *(one[2] for one in new))

    all_of, cut = P(None, None, None), P(None, "dp", None)
    return jax.shard_map(
        step,
        mesh=mesh,
        in_specs=(P(("rep", "dp"), None, None, None),) * 3 + (all_of,) * 3 + (cut,) * 6,
        out_specs=(P("rep", None, None),) * 3 + (P("rep", "dp", None),) * 6,
        check_vma=False,
    )
```

time: 387 us -> 372 us (0.961)
  local copies, waits for them, and re-layouts: 26.3 us -> 0.51 us
  Pallas kernels: 347 us -> 362 us
  other arithmetic: 11.8 us -> 7.54 us
    unnamed x23 -> x0, local copies, waits for them, and re-layouts: 25.1 us -> none
    pallas_call x2 -> x5, Pallas kernels: 347 us -> 362 us  [the longest x1 177 us: scatter(): pl.pallas_call(scatter_kernel, out_shape=[pltpu.VMEM((LAYERS, *b), BF16)...]
    convert_element_type x2, other arithmetic: 11.8 us -> 7.54 us  [adamw(): return ((w - 0.02 * step).astype(jnp.bfloat16), m, v)]
where the time goes in v3:
time: 372 us
  Pallas kernels  362 us (97%)
  other arithmetic  7.54 us (2%)
    pallas_call x1, Pallas kernels, scatter(): pl.pallas_call(scatter_kernel, out_shape=[pltpu.VMEM((LAYERS, *b), BF16)...  177 us
    pallas_call x1, Pallas kernels, gather(): pl.pallas_call(gather_kernel, out_shape=[pltpu.VMEM((LAYERS, 2, 2, 2, 2,...  167 us
    pallas_call x3, Pallas kernels, gather(): pl.pallas_call(land_kernel, out_shape=jax.ShapeDtypeStruct(t.shape, BF16)...  18.5 us
    convert_element_type x2, other arithmetic, adamw(): return ((w - 0.02 * step).astype(jnp.bfloat16), m, v)  7.54 us

profile of v3, /device:TPU:0, one launch (start us, length us, event | category | flops | bytes accessed | tf_op | source)
XLA Modules:
  0.0 371.5 jit_solution(8599734471263006971)
XLA Ops:
  0.6 176.6 %scatter.1 = (bf16[2,64,4096]{2,1,0:T(8,128)(2,1)S(1)}, bf16[2,64,4096]{2,1,0:T(8,128)(2,1)S(1)}, bf16[2,256,1024]{2,1,0:T(8,128)(2,1)S(1)}, f32[8,128]{1,0:T(8,...) custom-call(bf16[2,2,2,2,2,64,4096]{6,5,4,3,2,1,0:T(8,128)(2,1)} %bi, ...), custom_call_target="tpu_custom_call" | custom-call | tf_op jit(solution)/shard_map/scatter/pallas_call | solution.py:213
  177.3 0.5 slice.3
  178.5 4.3 %fusion.2 = (bf16[2,64,4096]{2,1,0:T(8,128)(2,1)S(1)}, f32[2,64,4096]{2,1,0:T(8,128)}, f32[2,64,4096]{2,1,0:T(8,128)}, bf16[2,64,4096]{2,1,0:T(8,128)(2,1)S(1)},...) fusion(bf16[2,64,4096]{2,1,0:T(8,128)(2,1)S(1)} %get-tuple-element.25, f32[]{:T(128)} %bitcast.6, ...), kind=kLoop, calls=%fused_computation.11 | loop fusion | flops 17825792 | bytes 23068676 | tf_op jit(solution)/shard_map/convert_element_type | solution.py:29
  182.8 3.3 fusion.8
  186.0 166.9 %gather.1 = (bf16[2,2,2,2,2,64,4096]{6,5,4,3,2,1,0:T(8,128)(2,1)S(1)}, bf16[2,2,2,2,2,64,4096]{6,5,4,3,2,1,0:T(8,128)(2,1)S(1)}, bf16[2,2,2,2,2,256,1024]{6,5,4,3,2,1,0:T(8,128)(2,1)S(1)}) custom-call(bf16[2,64,4096]{2,1,0:T(8,128)(2,1)S(1)} %get-tuple-element.47.refs_0_, bf16[2,64,4096]{2,1,0:T(8,128)(2,1)S(1)} %get-tuple-element.50.refs_1_, ...), custom_call_target="tpu_custom_call" | custom-call | tf_op jit(solution)/shard_map/gather/pallas_call | solution.py:306
  353.0 6.2 %land.3 = bf16[2,2,2,2,2,64,4096]{6,5,4,3,2,1,0:T(8,128)(2,1)} custom-call(bf16[2,2,2,2,2,64,4096]{6,5,4,3,2,1,0:T(8,128)(2,1)S(1)} %get-tuple-element.38.held), custom_call_target="tpu_custom_call" | custom-call | tf_op jit(solution)/shard_map/land/pallas_call | solution.py:316
  359.2 6.2 %land.4 = bf16[2,2,2,2,2,64,4096]{6,5,4,3,2,1,0:T(8,128)(2,1)} custom-call(bf16[2,2,2,2,2,64,4096]{6,5,4,3,2,1,0:T(8,128)(2,1)S(1)} %get-tuple-element.39.held), custom_call_target="tpu_custom_call" | custom-call | tf_op jit(solution)/shard_map/land/pallas_call | solution.py:316
  365.3 6.2 %land.5 = bf16[2,2,2,2,2,256,1024]{6,5,4,3,2,1,0:T(8,128)(2,1)} custom-call(bf16[2,2,2,2,2,256,1024]{6,5,4,3,2,1,0:T(8,128)(2,1)S(1)} %get-tuple-element.40.held), custom_call_target="tpu_custom_call" | custom-call | tf_op jit(solution)/shard_map/land/pallas_call | solution.py:316

commit v4 on v3

v4 whole, which is shorter than its diff:
```python
import functools

import jax
import jax.numpy as jnp
from jax import lax
from jax.experimental import pallas as pl
from jax.experimental.pallas import tpu as pltpu
from jax.sharding import PartitionSpec as P

MESH = pl.DeviceIdType.MESH
BF16, F32 = jnp.bfloat16, jnp.float32
DEVICES = 16
LAYERS = 2
CHUNKS = 4
JOBS = LAYERS * CHUNKS
FINE = 4
ITEMS = JOBS - 1 + FINE
SLOTS, AHEAD = 5, 3
LAGS = (1, 3, 5)
GATHER_CHUNKS = 4
GATHER_TAIL = 4
GATHER_JOBS = LAYERS * GATHER_CHUNKS
SCATTER_VMEM = 43
UPDATE_COLS, UPDATE_PARTS = 4096, 2
ORDERS = ("xyz", "yzx", "zxy")
STEP = {"x": 8, "y": 4, "z": 2, "c": 1}


def adamw(w, m, v, g):
    m = 0.9 * m + 0.1 * g
    v = 0.95 * v + 0.05 * g * g
    step = m * lax.rsqrt(v + 1e-8) + 0.1 * w
    return (w - 0.02 * step).astype(jnp.bfloat16), m, v


def place(me):
    bit = {a: (me // s) % 2 for a, s in STEP.items()}
    peer = {a: me + s - 2 * s * bit[a] for a, s in STEP.items()}
    return bit, peer


def greet_near(peer):
    barrier = pltpu.get_barrier_semaphore()
    for one in peer.values():
        pl.semaphore_signal(barrier, inc=1, device_id={"dp": one}, device_id_type=MESH)
    pl.semaphore_wait(barrier, len(peer))


def send(src, dst, sems, to):
    return pltpu.make_async_remote_copy(src, dst, sems[0], sems[1], device_id={"dp": to}, device_id_type=MESH)


def at_axis(ref, lead, axes, axis, bit):
    where = tuple(bit if a == axis else slice(None) for a in axes)
    return ref.at[(*lead, *where)]


def scatter_kernel(*refs):
    g, w, moments, refs = refs[:3], refs[3:6], refs[6:12], refs[12:]
    gb, total, own_w, held, refs = refs[:3], refs[3], refs[4:7], refs[7:13], refs[13:]
    own, s0, r1, r2, r3, acc = (refs[3 * i : 3 * i + 3] for i in range(6))
    mine, all_sq, own_sem, tx, rx, sq_tx, sq_rx, held_sem, free = refs[18:]
    me = lax.axis_index("dp")
    bit, peer = place(me)

    class Item:
        def __init__(self, i, fine):
            self.i, self.fine = i, fine
            self.j = 0 if fine else i - FINE + 1

        def part(self, k):
            h, w = r3[k].shape[-2:]
            if not self.fine:
                return pl.ds(0, h), pl.ds(0, w)
            if k == 2:
                return pl.ds(self.i * (h // FINE), h // FINE), pl.ds(0, w)
            return pl.ds(0, h), pl.ds(pl.multiple_of(self.i * (w // FINE), w // FINE), w // FINE)

        def piece(self, k):
            h = r3[k].shape[-2]
            rows, cols = self.part(k)
            return self.j // CHUNKS, pl.ds((self.j % CHUNKS) * h + rows.start, rows.size), cols

        def at(self, k, ref, lead, *where):
            return ref.at[(lead, *where, *self.part(k))]

        def own_copy(self, k):
            layer, rows, cols = self.piece(k)
            mine = self.at(k, own[k], self.i % 2, *[slice(None)] * 3)
            return pltpu.make_async_copy(g[k].at[layer, :, :, :, bit["c"], rows, cols], mine, own_sem.at[k, self.i])

        def hop(self, k, stage):
            sems = (tx.at[stage, k, self.i], rx.at[stage, k, self.i])
            a1, a2, a3 = ORDERS[k]
            every = slice(None)
            if stage == 0:
                layer, rows, cols = self.piece(k)
                theirs = self.at(k, s0[k], self.i % SLOTS, every, every, every)
                return send(g[k].at[layer, :, :, :, 1 - bit["c"], rows, cols], theirs, sems, peer["c"])
            if stage == 1:
                half = [1 - bit[a] if a == a1 else every for a in "xyz"]
                return send(self.at(k, s0[k], self.i % SLOTS, *half), self.at(k, r1[k], self.j, every, every), sems, peer[a1])
            if stage == 2:
                half = [1 - bit[a] if a == a2 else every for a in "xyz" if a != a1]
                return send(self.at(k, r1[k], self.j, *half), self.at(k, r2[k], self.j, every), sems, peer[a2])
            return send(self.at(k, r2[k], self.j, 1 - bit[a3]), self.at(k, r3[k], self.j), sems, peer[a3])

        def fetch(self):
            for k in range(3):
                self.own_copy(k).start()

        def cross(self):
            for k in range(3):
                self.hop(k, 0).start()

        def add_core(self):
            for k in range(3):
                self.own_copy(k).wait()
                self.hop(k, 0).wait_recv()

                @pl.loop(0, 2 if self.fine else 8)
                def _(b):
                    at = (b, slice(None), slice(None)) if self.fine else (b // 4, (b // 2) % 2, b % 2)
                    at = (*at, *self.part(k))
                    slot = (self.i % SLOTS, *at)
                    s0[k][slot] = plus(own[k][(self.i % 2, *at)], s0[k][slot])

                self.hop(k, 1).start()

        def add_first(self):
            for k in range(3):
                a1 = ORDERS[k][0]
                self.hop(k, 1).wait_recv()

                @pl.loop(0, 2 if self.fine else 4)
                def _(b):
                    at = [b, slice(None)] if self.fine else [b // 2, b % 2]
                    full = list(at)
                    full.insert("xyz".index(a1), bit[a1])
                    to = (self.j, *at, *self.part(k))
                    r1[k][to] = plus(s0[k][(self.i % SLOTS, *full, *self.part(k))], r1[k][to])

                self.hop(k, 2).start()
            for k in range(3):
                self.hop(k, 1).wait_send()

        def add_second(self):
            for k in range(3):
                a1, a2, _a3 = ORDERS[k]
                rest = [a for a in "xyz" if a != a1]
                self.hop(k, 2).wait_recv()

                @pl.loop(0, 2)
                def _(b):
                    full = [b]
                    full.insert(rest.index(a2), bit[a2])
                    to = (self.j, b, *self.part(k))
                    r2[k][to] = plus(r1[k][(self.j, *full, *self.part(k))], r2[k][to])

                self.hop(k, 3).start()

        def add_third(self):
            for k in range(3):
                self.hop(k, 3).wait_recv()
                done = plus(r2[k][(self.j, bit[ORDERS[k][2]], *self.part(k))], r3[k][(self.j, *self.part(k))])
                gb[k][self.piece(k)] = done
                wide = done.astype(F32)
                squares = wide * wide
                low = sum(squares[8 * i : 8 * i + 8] for i in range(done.shape[0] // 8))
                acc[k][...] += sum(low[:, 128 * i : 128 * i + 128] for i in range(low.shape[1] // 128))

        def drain(self):
            for k in range(3):
                for stage in (0, 2, 3):
                    self.hop(k, stage).wait_send()

    def plus(a, b):
        return (a.astype(F32) + b.astype(F32)).astype(BF16)

    def do(i, what):
        @pl.when((i >= 0) & (i < FINE))
        def _():
            getattr(Item(i, True), what)()

        @pl.when((i >= FINE) & (i < ITEMS))
        def _():
            getattr(Item(i, False), what)()

    staged = [pltpu.make_async_copy(w[k].at[:, bit["x"], bit["y"], bit["z"], bit["c"]], own_w[k], held_sem.at[k]) for k in range(3)]
    staged += [pltpu.make_async_copy(moments[i], held[i], held_sem.at[3 + i]) for i in range(6)]

    Item(0, True).fetch()
    greet_near(peer)
    for i in range(AHEAD):
        Item(i, True).cross()
    for k in range(3):
        acc[k][...] = jnp.zeros_like(acc[k])

    def turn(s, _):
        @pl.when((s >= SLOTS - AHEAD) & (s < ITEMS - AHEAD))
        def _():
            pl.semaphore_wait(free, 1)

        do(s + AHEAD, "cross")
        do(s + 1, "fetch")

        @pl.when(s == FINE)
        def _():
            for one in staged:
                one.start()

        do(s, "add_core")
        do(s - LAGS[0], "add_first")

        @pl.when((s >= LAGS[0]) & (s < LAGS[0] + ITEMS - SLOTS))
        def _():
            pl.semaphore_signal(free, inc=1, device_id={"dp": peer["c"]}, device_id_type=MESH)

        do(s - LAGS[1], "add_second")
        do(s - LAGS[2], "add_third")
        return 0

    lax.fori_loop(0, ITEMS + LAGS[2], turn, 0)

    part = jnp.zeros((8, 128), F32)
    for k in range(3):
        part += acc[k][...]
    part = jnp.sum(part, axis=0, keepdims=True)
    mine[...] = part
    all_sq[me] = part
    sends = [send(mine, all_sq.at[me], (sq_tx.at[i], sq_rx.at[i]), (me + i) % DEVICES) for i in range(1, DEVICES)]
    for one in sends:
        one.start()

    def drain(i, _):
        do(i, "drain")
        return 0

    lax.fori_loop(0, ITEMS, drain, 0)
    for one in staged:
        one.wait()
    for one in sends:
        one.wait()
    total[...] = jnp.full((8, 128), jnp.sum(sum(all_sq[i] for i in range(DEVICES))), F32)


def scatter(terms, weights, moments):
    blocks = [(t.shape[1] // DEVICES, t.shape[2]) for t in terms]
    split = [t.reshape(LAYERS, 2, 2, 2, 2, *b) for t, b in zip((*terms, *weights), (*blocks, *blocks), strict=True)]
    pieces = [(r // CHUNKS, c) for r, c in blocks]
    sem = pltpu.SemaphoreType.DMA
    leads = ((2, 2, 2, 2), (SLOTS, 2, 2, 2), (JOBS, 2, 2), (JOBS, 2), (JOBS,))
    scratch = [pltpu.VMEM((*lead, *p), BF16) for lead in leads for p in pieces]
    scratch += [pltpu.VMEM((8, 128), F32)] * 3
    scratch += [pltpu.VMEM((1, 128), F32), pltpu.VMEM((DEVICES, 1, 128), F32)]
    scratch += [sem((3, ITEMS)), sem((4, 3, ITEMS)), sem((4, 3, ITEMS)), sem((DEVICES,)), sem((DEVICES,)), sem((9,)), pltpu.SemaphoreType.REGULAR]
    sums_0, sums_1, sums_2, total, *held = pl.pallas_call(
        scatter_kernel,
        out_shape=[pltpu.VMEM((LAYERS, *b), BF16) for b in blocks] + [pltpu.VMEM((8, 128), F32)] + [pltpu.VMEM((LAYERS, *b), BF16) for b in blocks] + [pltpu.VMEM(m.shape, F32) for m in moments],
        in_specs=[pl.BlockSpec(memory_space=pltpu.HBM)] * 12,
        out_specs=[pl.BlockSpec(memory_space=pltpu.VMEM)] * 13,
        scratch_shapes=scratch,
        compiler_params=pltpu.CompilerParams(collective_id=0, has_side_effects=True, vmem_limit_bytes=SCATTER_VMEM * 2**20),
        name="scatter",
    )(*split, *moments)
    return (sums_0, sums_1, sums_2), total, held[:3], held[3:6], held[6:]


def update_kernel(*refs):
    g, w, m, v, total = refs[:3], refs[3:6], refs[6:9], refs[9:12], refs[12]
    new_w, out_m, out_v, refs = refs[13:16], refs[16:19], refs[19:22], refs[22:]
    new_m, new_v, sem = refs[:3], refs[3:6], refs[6]
    count = DEVICES * sum(LAYERS * r.shape[1] * r.shape[2] for r in g)
    factor = jnp.minimum(1.0, 0.5 * lax.rsqrt(total[...] / count + 1e-30))[:1, :1]
    copies = []
    for k in range(3):
        rows = 16 * UPDATE_COLS // g[k].shape[2]
        steps = g[k].shape[1] // rows

        for layer in range(LAYERS):
            for half in range(UPDATE_PARTS):
                part = steps // UPDATE_PARTS

                @pl.loop(half * part, (half + 1) * part)
                def _(i):
                    at = (layer, pl.ds(pl.multiple_of(i * rows, rows), rows))
                    new_w[k][at], new_m[k][at], new_v[k][at] = adamw(w[k][at].astype(F32), m[k][at], v[k][at], g[k][at].astype(F32) * factor)

                done = (layer, pl.ds(half * part * rows, part * rows))
                for new, out in ((new_m[k], out_m[k]), (new_v[k], out_v[k])):
                    copies.append(pltpu.make_async_copy(new.at[done], out.at[done], sem.at[len(copies)]))
                    copies[-1].start()
    for one in copies:
        one.wait()


def update(g, w, m, v, total):
    moments = [jax.ShapeDtypeStruct(one.shape, F32) for one in (*m, *v)]
    out = pl.pallas_call(
        update_kernel,
        out_shape=[pltpu.VMEM(one.shape, BF16) for one in w] + moments,
        in_specs=[pl.BlockSpec(memory_space=pltpu.VMEM)] * 13,
        out_specs=[pl.BlockSpec(memory_space=pltpu.VMEM)] * 3 + [pl.BlockSpec(memory_space=pltpu.HBM)] * 6,
        scratch_shapes=[pltpu.VMEM(one.shape, F32) for one in moments] + [pltpu.SemaphoreType.DMA((6 * LAYERS * UPDATE_PARTS,))],
        compiler_params=pltpu.CompilerParams(vmem_limit_bytes=14 * 2**20),
        name="update",
    )(*g, *w, *m, *v, total)
    return out[:3], out[3:6], out[6:]


def gather_kernel(*refs):
    w, refs = refs[:3], refs[3:]
    whole, (own_tx, own_rx, tx, rx, ftx, frx, last_tx, last_rx) = refs[:3], refs[3:]
    me = lax.axis_index("dp")
    bit, peer = place(me)
    heights = [r.shape[-2] // GATHER_CHUNKS for r in whole]

    def region(k, j, bits):
        h = heights[k]
        where = tuple(bits.get(a, slice(None)) for a in "xyz")
        return whole[k].at[(j // GATHER_CHUNKS, *where, bit["c"], pl.ds((j % GATHER_CHUNKS) * h, h))]

    def hop(k, stage, j):
        axes = ORDERS[k][: 3 - stage]
        part = region(k, j, {a: bit[a] for a in axes})
        if stage == 0:
            h = heights[k]
            source = w[k].at[j // GATHER_CHUNKS, pl.ds((j % GATHER_CHUNKS) * h, h)]
        else:
            source = part
        return send(source, part, (tx.at[stage, k, j], rx.at[stage, k, j]), peer[ORDERS[k][2 - stage]])

    def forward(k, stage, j):
        bits = {a: bit[a] for a in ORDERS[k][: 3 - stage]}
        axis = ORDERS[k][2 - stage]
        bits[axis] = 1 - bit[axis]
        part = region(k, j, bits)
        return send(part, part, (ftx.at[stage, k, j], frx.at[stage, k, j]), peer["c"])

    def last_hop(k, q, forward):
        axis = ORDERS[k][0]
        h = heights[k] // GATHER_TAIL if k == 2 else heights[k]
        w = whole[k].shape[-1] // (1 if k == 2 else GATHER_TAIL)
        row, col = (GATHER_CHUNKS - 1) * heights[k] + (q * h if k == 2 else 0), 0 if k == 2 else q * w
        where = tuple((1 - bit[axis] if forward else bit[axis]) if a == axis else slice(None) for a in "xyz")
        part = whole[k].at[(LAYERS - 1, *where, bit["c"], pl.ds(row, h), pl.ds(col, w))]
        way = int(forward)
        return send(part, part, (last_tx.at[way, k, q], last_rx.at[way, k, q]), peer["c" if forward else axis])

    def own_forward(k):
        part = whole[k].at[:, bit["x"], bit["y"], bit["z"], bit["c"]]
        return send(w[k], part, (own_tx.at[k], own_rx.at[k]), peer["c"])

    greet_near(peer)

    def first(j, _):
        for k in range(3):
            hop(k, 0, j).start()
        return 0

    lax.fori_loop(0, GATHER_JOBS, first, 0)
    for k in range(3):
        own_forward(k).start()
    for k in range(3):
        whole[k][:, bit["x"], bit["y"], bit["z"], bit["c"]] = w[k][...]

    def turn(s, _):
        for stage in range(3):
            end = GATHER_JOBS - 1 if stage == 2 else GATHER_JOBS

            @pl.when((s >= stage) & (s < end + stage))
            def _():
                j = s - stage
                for k in range(3):
                    hop(k, stage, j).wait_recv()
                    if stage == 0:
                        hop(k, 1, j).start()
                    if stage == 1:

                        @pl.when(j < GATHER_JOBS - 1)
                        def _():
                            hop(k, 2, j).start()

                        @pl.when(j == GATHER_JOBS - 1)
                        def _():
                            for q in range(GATHER_TAIL):
                                last_hop(k, q, False).start()

                    forward(k, stage, j).start()

        return 0

    lax.fori_loop(0, GATHER_JOBS + 1, turn, 0)
    for q in range(GATHER_TAIL):
        for k in range(3):
            last_hop(k, q, False).wait_recv()
            last_hop(k, q, True).start()

    def drain(j, _):
        for k in range(3):
            for stage in range(3):
                hop(k, stage, j).wait_send()
                forward(k, stage, j).wait()
        return 0

    lax.fori_loop(0, GATHER_JOBS - 1, drain, 0)
    for k in range(3):
        for stage in range(2):
            hop(k, stage, GATHER_JOBS - 1).wait_send()
            forward(k, stage, GATHER_JOBS - 1).wait()
        own_forward(k).wait()
        for q in range(GATHER_TAIL):
            last_hop(k, q, False).wait_send()
            last_hop(k, q, True).wait()


def land_kernel(held, out, sem):
    copies = [pltpu.make_async_copy(held.at[l, x], out.at[l, x], sem.at[2 * l + x]) for l in range(LAYERS) for x in range(2)]
    for one in copies:
        one.start()
    for one in copies:
        one.wait()


def gather(blocks):
    shapes = [b.shape[1:] for b in blocks]
    sem = pltpu.SemaphoreType.DMA
    whole = pl.pallas_call(
        gather_kernel,
        out_shape=[pltpu.VMEM((LAYERS, 2, 2, 2, 2, *s), BF16) for s in shapes],
        in_specs=[pl.BlockSpec(memory_space=pltpu.VMEM)] * 3,
        out_specs=[pl.BlockSpec(memory_space=pltpu.VMEM)] * 3,
        scratch_shapes=[sem((3,))] * 2 + [sem((3, 3, GATHER_JOBS))] * 4 + [sem((2, 3, GATHER_TAIL))] * 2,
        compiler_params=pltpu.CompilerParams(collective_id=1, has_side_effects=True, vmem_limit_bytes=2**20),
        name="gather",
    )(*blocks)
    landed = [
        pl.pallas_call(
            land_kernel,
            out_shape=jax.ShapeDtypeStruct(t.shape, BF16),
            in_specs=[pl.BlockSpec(memory_space=pl.ANY)],
            out_specs=pl.BlockSpec(memory_space=pltpu.HBM),
            scratch_shapes=[sem((4,))],
            compiler_params=pltpu.CompilerParams(vmem_limit_bytes=2**19),
            name="land",
        )(t)
        for t in whole
    ]
    return [t.reshape(LAYERS, DEVICES * s[0], s[1]) for t, s in zip(landed, shapes, strict=True)]


def solution(mesh):
    def step(*arrays):
        terms, weights, m, v = (arrays[i : i + 3] for i in (0, 3, 6, 9))
        sums, total, own, m, v = scatter([t[0] for t in terms], weights, (*m, *v))
        new, m, v = update(sums, own, m, v, total)
        whole = gather(new)
        return (*whole, *m, *v)

    all_of, cut = P(None, None, None), P(None, "dp", None)
    return jax.shard_map(
        step,
        mesh=mesh,
        in_specs=(P(("rep", "dp"), None, None, None),) * 3 + (all_of,) * 3 + (cut,) * 6,
        out_specs=(P("rep", None, None),) * 3 + (P("rep", "dp", None),) * 6,
        check_vma=False,
    )
```

time: 372 us -> 363 us (0.976)
  other arithmetic: 7.54 us -> 0 us
    convert_element_type x2 -> x0, other arithmetic: 7.54 us -> none  [adamw(): return ((w - 0.02 * step).astype(jnp.bfloat16), m, v)]
    pallas_call x0 -> x1, Pallas kernels: none -> 5.34 us  [update(): pl.pallas_call(update_kernel, out_shape=[pltpu.VMEM(one.shape, BF16) for...]
    pallas_call x1, Pallas kernels: 177 us -> 172 us  [scatter(): pl.pallas_call(scatter_kernel, out_shape=[pltpu.VMEM((LAYERS, *b), BF16)...]
where the time goes in v4:
time: 363 us; the launch traced here: 362 us
  Pallas kernels  360 us (99%)
    pallas_call x1, Pallas kernels, scatter(): pl.pallas_call(scatter_kernel, out_shape=[pltpu.VMEM((LAYERS, *b), BF16)...  172 us
    pallas_call x1, Pallas kernels, gather(): pl.pallas_call(gather_kernel, out_shape=[pltpu.VMEM((LAYERS, 2, 2, 2, 2,...  164 us
    pallas_call x3, Pallas kernels, gather(): pl.pallas_call(land_kernel, out_shape=jax.ShapeDtypeStruct(t.shape, BF16)...  17.9 us

profile of v4, /device:TPU:0, one launch (start us, length us, event | category | flops | bytes accessed | tf_op | source)
XLA Modules:
  0.0 362.5 jit_solution(11751077810907710530)
XLA Ops:
  0.6 172.2 %scatter.1 = (bf16[2,64,4096]{2,1,0:T(8,128)(2,1)S(1)}, bf16[2,64,4096]{2,1,0:T(8,128)(2,1)S(1)}, bf16[2,256,1024]{2,1,0:T(8,128)(2,1)S(1)}, f32[8,128]{1,0:T(8,...) custom-call(bf16[2,2,2,2,2,64,4096]{6,5,4,3,2,1,0:T(8,128)(2,1)} %bi, ...), custom_call_target="tpu_custom_call" | custom-call | tf_op jit(solution)/shard_map/scatter/pallas_call | solution.py:257
  172.9 5.3 %update.1 = (bf16[2,64,4096]{2,1,0:T(8,128)(2,1)S(1)}, bf16[2,64,4096]{2,1,0:T(8,128)(2,1)S(1)}, bf16[2,256,1024]{2,1,0:T(8,128)(2,1)S(1)}, f32[2,64,4096]{2,1,0...) custom-call(bf16[2,64,4096]{2,1,0:T(8,128)(2,1)S(1)} %get-tuple-elem, ...), custom_call_target="tpu_custom_call" | custom-call | tf_op jit(solution)/shard_map/update/pallas_call | solution.py:299
  178.2 0.0 copy-start
  178.3 1.0 copy-done
  179.2 0.0 copy-start.1
  179.2 1.2 copy-done.1
  180.4 164.1 %gather.1 = (bf16[2,2,2,2,2,64,4096]{6,5,4,3,2,1,0:T(8,128)(2,1)S(1)}, bf16[2,2,2,2,2,64,4096]{6,5,4,3,2,1,0:T(8,128)(2,1)S(1)}, bf16[2,2,2,2,2,256,1024]{6,5,4,3,2,1,0:T(8,128)(2,1)S(1)}) custom-call(bf16[2,64,4096]{2,1,0:T(8,128)(2,1)S(1)} %get-tuple-element.47.refs_0_, bf16[2,64,4096]{2,1,0:T(8,128)(2,1)S(1)} %get-tuple-element.48.refs_1_, ...), custom_call_target="tpu_custom_call" | custom-call | tf_op jit(solution)/shard_map/gather/pallas_call | solution.py:428
  344.6 6.0 %land.3 = bf16[2,2,2,2,2,64,4096]{6,5,4,3,2,1,0:T(8,128)(2,1)} custom-call(bf16[2,2,2,2,2,64,4096]{6,5,4,3,2,1,0:T(8,128)(2,1)S(1)} %get-tuple-element.50.held), custom_call_target="tpu_custom_call" | custom-call | tf_op jit(solution)/shard_map/land/pallas_call | solution.py:438
  350.6 6.0 %land.4 = bf16[2,2,2,2,2,64,4096]{6,5,4,3,2,1,0:T(8,128)(2,1)} custom-call(bf16[2,2,2,2,2,64,4096]{6,5,4,3,2,1,0:T(8,128)(2,1)S(1)} %get-tuple-element.51.held), custom_call_target="tpu_custom_call" | custom-call | tf_op jit(solution)/shard_map/land/pallas_call | solution.py:438
  356.5 6.0 %land.5 = bf16[2,2,2,2,2,256,1024]{6,5,4,3,2,1,0:T(8,128)(2,1)} custom-call(bf16[2,2,2,2,2,256,1024]{6,5,4,3,2,1,0:T(8,128)(2,1)S(1)} %get-tuple-element.52.held), custom_call_target="tpu_custom_call" | custom-call | tf_op jit(solution)/shard_map/land/pallas_call | solution.py:438
Async XLA Ops:
  178.2 1.0 copy-start
  179.2 1.2 copy-start.1

commit v5 on v4

--- a/solution.py
+++ b/solution.py
@@ -17,10 +17,10 @@
 ITEMS = JOBS - 1 + FINE
 SLOTS, AHEAD = 5, 3
 LAGS = (1, 3, 5)
-GATHER_CHUNKS = 4
-GATHER_TAIL = 4
+GATHER_CHUNKS = 2
+GATHER_TAIL = 8
 GATHER_JOBS = LAYERS * GATHER_CHUNKS
-SCATTER_VMEM = 43
+SCATTER_VMEM, LAND_VMEM = 44_700_000, 4 * 2**20
 UPDATE_COLS, UPDATE_PARTS = 4096, 2
 ORDERS = ("xyz", "yzx", "zxy")
 STEP = {"x": 8, "y": 4, "z": 2, "c": 1}
@@ -260,7 +260,7 @@
         in_specs=[pl.BlockSpec(memory_space=pltpu.HBM)] * 12,
         out_specs=[pl.BlockSpec(memory_space=pltpu.VMEM)] * 13,
         scratch_shapes=scratch,
-        compiler_params=pltpu.CompilerParams(collective_id=0, has_side_effects=True, vmem_limit_bytes=SCATTER_VMEM * 2**20),
+        compiler_params=pltpu.CompilerParams(collective_id=0, has_side_effects=True, vmem_limit_bytes=SCATTER_VMEM),
         name="scatter",
     )(*split, *moments)
     return (sums_0, sums_1, sums_2), total, held[:3], held[3:6], held[6:]
@@ -414,8 +414,9 @@
             last_hop(k, q, True).wait()
 
 
-def land_kernel(held, out, sem):
-    copies = [pltpu.make_async_copy(held.at[l, x], out.at[l, x], sem.at[2 * l + x]) for l in range(LAYERS) for x in range(2)]
+def land_kernel(*refs):
+    held, out, sem = refs[:3], refs[3:6], refs[6]
+    copies = [pltpu.make_async_copy(held[k].at[l, x], out[k].at[l, x], sem.at[k, l, x]) for k in range(3) for l in range(LAYERS) for x in range(2)]
     for one in copies:
         one.start()
     for one in copies:
@@ -434,18 +435,15 @@
         compiler_params=pltpu.CompilerParams(collective_id=1, has_side_effects=True, vmem_limit_bytes=2**20),
         name="gather",
     )(*blocks)
-    landed = [
-        pl.pallas_call(
-            land_kernel,
-            out_shape=jax.ShapeDtypeStruct(t.shape, BF16),
-            in_specs=[pl.BlockSpec(memory_space=pl.ANY)],
-            out_specs=pl.BlockSpec(memory_space=pltpu.HBM),
-            scratch_shapes=[sem((4,))],
-            compiler_params=pltpu.CompilerParams(vmem_limit_bytes=2**19),
-            name="land",
-        )(t)
-        for t in whole
-    ]
+    landed = pl.pallas_call(
+        land_kernel,
+        out_shape=[jax.ShapeDtypeStruct(one.shape, BF16) for one in whole],
+        in_specs=[pl.BlockSpec(memory_space=pltpu.VMEM)] * 3,
+        out_specs=[pl.BlockSpec(memory_space=pltpu.HBM)] * 3,
+        scratch_shapes=[sem((3, LAYERS, 2))],
+        compiler_params=pltpu.CompilerParams(vmem_limit_bytes=LAND_VMEM),
+        name="land",
+    )(*whole)
     return [t.reshape(LAYERS, DEVICES * s[0], s[1]) for t, s in zip(landed, shapes, strict=True)]
 
 

time: 363 us -> 358 us (0.986)
    pallas_call x3 -> x1, Pallas kernels: 17.9 us -> 16.1 us  [gather(): pl.pallas_call(land_kernel, out_shape=[jax.ShapeDtypeStruct(one.shape, BF...]
where the time goes in v5:
time: 358 us
  Pallas kernels  357 us (100%)
    pallas_call x1, Pallas kernels, scatter(): pl.pallas_call(scatter_kernel, out_shape=[pltpu.VMEM((LAYERS, *b), BF16)...  172 us
    pallas_call x1, Pallas kernels, gather(): pl.pallas_call(gather_kernel, out_shape=[pltpu.VMEM((LAYERS, 2, 2, 2, 2,...  163 us
    pallas_call x1, Pallas kernels, gather(): pl.pallas_call(land_kernel, out_shape=[jax.ShapeDtypeStruct(one.shape, BF...  16.1 us

profile of v5, /device:TPU:0, one launch (start us, length us, event | category | flops | bytes accessed | tf_op | source)
XLA Modules:
  0.0 357.7 jit_solution(6510613431111233939)
XLA Ops:
  0.6 172.2 %scatter.1 = (bf16[2,64,4096]{2,1,0:T(8,128)(2,1)S(1)}, bf16[2,64,4096]{2,1,0:T(8,128)(2,1)S(1)}, bf16[2,256,1024]{2,1,0:T(8,128)(2,1)S(1)}, f32[8,128]{1,0:T(8,...) custom-call(bf16[2,2,2,2,2,64,4096]{6,5,4,3,2,1,0:T(8,128)(2,1)} %bi, ...), custom_call_target="tpu_custom_call" | custom-call | tf_op jit(solution)/shard_map/scatter/pallas_call | solution.py:257
  172.9 5.3 %update.1 = (bf16[2,64,4096]{2,1,0:T(8,128)(2,1)S(1)}, bf16[2,64,4096]{2,1,0:T(8,128)(2,1)S(1)}, bf16[2,256,1024]{2,1,0:T(8,128)(2,1)S(1)}, f32[2,64,4096]{2,1,0...) custom-call(bf16[2,64,4096]{2,1,0:T(8,128)(2,1)S(1)} %get-tuple-elem, ...), custom_call_target="tpu_custom_call" | custom-call | tf_op jit(solution)/shard_map/update/pallas_call | solution.py:299
  178.3 163.4 %gather.1 = (bf16[2,2,2,2,2,64,4096]{6,5,4,3,2,1,0:T(8,128)(2,1)S(1)}, bf16[2,2,2,2,2,64,4096]{6,5,4,3,2,1,0:T(8,128)(2,1)S(1)}, bf16[2,2,2,2,2,256,1024]{6,5,4,3,2,1,0:T(8,128)(2,1)S(1)}) custom-call(bf16[2,64,4096]{2,1,0:T(8,128)(2,1)S(1)} %get-tuple-element.50.refs_0_, bf16[2,64,4096]{2,1,0:T(8,128)(2,1)S(1)} %get-tuple-element.51.refs_1_, ...), custom_call_target="tpu_custom_call" | custom-call | tf_op jit(solution)/shard_map/gather/pallas_call | solution.py:429
  341.6 16.1 %land.1 = (bf16[2,2,2,2,2,64,4096]{6,5,4,3,2,1,0:T(8,128)(2,1)}, bf16[2,2,2,2,2,64,4096]{6,5,4,3,2,1,0:T(8,128)(2,1)}, bf16[2,2,2,2,2,256,1024]{6,5,4,3,2,1,0:T(8,128)(2,1)}) custom-call(bf16[2,2,2,2,2,64,4096]{6,5,4,3,2,1,0:T(8,128)(2,1)S(1)} %get-tuple-element.53.refs_0_, bf16[2,2,2,2,2,64,4096]{6,5,4,3,2,1,0:T(8,128)(2,1)S(1)} %get-tuple-element.54.refs_1_, ...), custom_call_target="tpu_custom_call" | custom-call | tf_op jit(solution)/shard_map/land/pallas_call | solution.py:438

commit v6 on v5

--- a/solution.py
+++ b/solution.py
@@ -17,7 +17,7 @@
 ITEMS = JOBS - 1 + FINE
 SLOTS, AHEAD = 5, 3
 LAGS = (1, 3, 5)
-GATHER_CHUNKS = 2
+GATHER_CHUNKS = 1
 GATHER_TAIL = 8
 GATHER_JOBS = LAYERS * GATHER_CHUNKS
 SCATTER_VMEM, LAND_VMEM = 44_700_000, 4 * 2**20
@@ -26,11 +26,10 @@
 STEP = {"x": 8, "y": 4, "z": 2, "c": 1}
 
 
-def adamw(w, m, v, g):
-    m = 0.9 * m + 0.1 * g
-    v = 0.95 * v + 0.05 * g * g
-    step = m * lax.rsqrt(v + 1e-8) + 0.1 * w
-    return (w - 0.02 * step).astype(jnp.bfloat16), m, v
+def adamw(w, m, v, h):
+    m = 0.9 * m + h
+    v = 0.95 * v + (5.0 * h) * h
+    return (0.998 * w - (0.02 * m) * lax.rsqrt(v + 1e-8)).astype(jnp.bfloat16), m, v
 
 
 def place(me):
@@ -272,6 +271,7 @@
     new_m, new_v, sem = refs[:3], refs[3:6], refs[6]
     count = DEVICES * sum(LAYERS * r.shape[1] * r.shape[2] for r in g)
     factor = jnp.minimum(1.0, 0.5 * lax.rsqrt(total[...] / count + 1e-30))[:1, :1]
+    tenth = 0.1 * factor
     copies = []
     for k in range(3):
         rows = 16 * UPDATE_COLS // g[k].shape[2]
@@ -284,7 +284,7 @@
                 @pl.loop(half * part, (half + 1) * part)
                 def _(i):
                     at = (layer, pl.ds(pl.multiple_of(i * rows, rows), rows))
-                    new_w[k][at], new_m[k][at], new_v[k][at] = adamw(w[k][at].astype(F32), m[k][at], v[k][at], g[k][at].astype(F32) * factor)
+                    new_w[k][at], new_m[k][at], new_v[k][at] = adamw(w[k][at].astype(F32), m[k][at], v[k][at], g[k][at].astype(F32) * tenth)
 
                 done = (layer, pl.ds(half * part * rows, part * rows))
                 for new, out in ((new_m[k], out_m[k]), (new_v[k], out_v[k])):

time: 358 us -> 358 us (level)
  no operation moved by 1% of the time
where the time goes in v6:
time: 358 us; the launch traced here: 357 us
  Pallas kernels  357 us (100%)
    pallas_call x1, Pallas kernels, scatter(): pl.pallas_call(scatter_kernel, out_shape=[pltpu.VMEM((LAYERS, *b), BF16)...  172 us
    pallas_call x1, Pallas kernels, gather(): pl.pallas_call(gather_kernel, out_shape=[pltpu.VMEM((LAYERS, 2, 2, 2, 2,...  163 us
    pallas_call x1, Pallas kernels, gather(): pl.pallas_call(land_kernel, out_shape=[jax.ShapeDtypeStruct(one.shape, BF...  16.1 us

profile of v6, /device:TPU:0, one launch (start us, length us, event | category | flops | bytes accessed | tf_op | source)
XLA Modules:
  0.0 357.5 jit_solution(15441446926261102952)
XLA Ops:
  0.6 172.2 %scatter.1 = (bf16[2,64,4096]{2,1,0:T(8,128)(2,1)S(1)}, bf16[2,64,4096]{2,1,0:T(8,128)(2,1)S(1)}, bf16[2,256,1024]{2,1,0:T(8,128)(2,1)S(1)}, f32[8,128]{1,0:T(8,...) custom-call(bf16[2,2,2,2,2,64,4096]{6,5,4,3,2,1,0:T(8,128)(2,1)} %bi, ...), custom_call_target="tpu_custom_call" | custom-call | tf_op jit(solution)/shard_map/scatter/pallas_call | solution.py:256
  172.9 5.2 %update.1 = (bf16[2,64,4096]{2,1,0:T(8,128)(2,1)S(1)}, bf16[2,64,4096]{2,1,0:T(8,128)(2,1)S(1)}, bf16[2,256,1024]{2,1,0:T(8,128)(2,1)S(1)}, f32[2,64,4096]{2,1,0...) custom-call(bf16[2,64,4096]{2,1,0:T(8,128)(2,1)S(1)} %get-tuple-elem, ...), custom_call_target="tpu_custom_call" | custom-call | tf_op jit(solution)/shard_map/update/pallas_call | solution.py:299
  178.1 163.3 %gather.1 = (bf16[2,2,2,2,2,64,4096]{6,5,4,3,2,1,0:T(8,128)(2,1)S(1)}, bf16[2,2,2,2,2,64,4096]{6,5,4,3,2,1,0:T(8,128)(2,1)S(1)}, bf16[2,2,2,2,2,256,1024]{6,5,4,3,2,1,0:T(8,128)(2,1)S(1)}) custom-call(bf16[2,64,4096]{2,1,0:T(8,128)(2,1)S(1)} %get-tuple-element.50.refs_0_, bf16[2,64,4096]{2,1,0:T(8,128)(2,1)S(1)} %get-tuple-element.51.refs_1_, ...), custom_call_target="tpu_custom_call" | custom-call | tf_op jit(solution)/shard_map/gather/pallas_call | solution.py:429
  341.4 16.1 %land.1 = (bf16[2,2,2,2,2,64,4096]{6,5,4,3,2,1,0:T(8,128)(2,1)}, bf16[2,2,2,2,2,64,4096]{6,5,4,3,2,1,0:T(8,128)(2,1)}, bf16[2,2,2,2,2,256,1024]{6,5,4,3,2,1,0:T(8,128)(2,1)}) custom-call(bf16[2,2,2,2,2,64,4096]{6,5,4,3,2,1,0:T(8,128)(2,1)S(1)} %get-tuple-element.53.refs_0_, bf16[2,2,2,2,2,64,4096]{6,5,4,3,2,1,0:T(8,128)(2,1)S(1)} %get-tuple-element.54.refs_1_, ...), custom_call_target="tpu_custom_call" | custom-call | tf_op jit(solution)/shard_map/land/pallas_call | solution.py:438

commit v7 on v6

--- a/solution.py
+++ b/solution.py
@@ -38,10 +38,12 @@
     return bit, peer
 
 
-def greet_near(peer):
+def greet_near(peer, meanwhile=None):
     barrier = pltpu.get_barrier_semaphore()
     for one in peer.values():
         pl.semaphore_signal(barrier, inc=1, device_id={"dp": one}, device_id_type=MESH)
+    if meanwhile:
+        meanwhile()
     pl.semaphore_wait(barrier, len(peer))
 
 
@@ -188,8 +190,7 @@
     staged = [pltpu.make_async_copy(w[k].at[:, bit["x"], bit["y"], bit["z"], bit["c"]], own_w[k], held_sem.at[k]) for k in range(3)]
     staged += [pltpu.make_async_copy(moments[i], held[i], held_sem.at[3 + i]) for i in range(6)]
 
-    Item(0, True).fetch()
-    greet_near(peer)
+    greet_near(peer, Item(0, True).fetch)
     for i in range(AHEAD):
         Item(i, True).cross()
     for k in range(3):

time: 358 us -> 358 us (level)
  no operation moved by 1% of the time
where the time goes in v7:
time: 358 us; the launch traced here: 357 us
  Pallas kernels  357 us (100%)
    pallas_call x1, Pallas kernels, scatter(): pl.pallas_call(scatter_kernel, out_shape=[pltpu.VMEM((LAYERS, *b), BF16)...  172 us
    pallas_call x1, Pallas kernels, gather(): pl.pallas_call(gather_kernel, out_shape=[pltpu.VMEM((LAYERS, 2, 2, 2, 2,...  163 us
    pallas_call x1, Pallas kernels, gather(): pl.pallas_call(land_kernel, out_shape=[jax.ShapeDtypeStruct(one.shape, BF...  16.1 us

profile of v7, /device:TPU:0, one launch (start us, length us, event | category | flops | bytes accessed | tf_op | source)
XLA Modules:
  0.0 357.5 jit_solution(2535508264756982331)
XLA Ops:
  0.6 172.2 %scatter.1 = (bf16[2,64,4096]{2,1,0:T(8,128)(2,1)S(1)}, bf16[2,64,4096]{2,1,0:T(8,128)(2,1)S(1)}, bf16[2,256,1024]{2,1,0:T(8,128)(2,1)S(1)}, f32[8,128]{1,0:T(8,...) custom-call(bf16[2,2,2,2,2,64,4096]{6,5,4,3,2,1,0:T(8,128)(2,1)} %bi, ...), custom_call_target="tpu_custom_call" | custom-call | tf_op jit(solution)/shard_map/scatter/pallas_call | solution.py:257
  172.9 5.2 %update.1 = (bf16[2,64,4096]{2,1,0:T(8,128)(2,1)S(1)}, bf16[2,64,4096]{2,1,0:T(8,128)(2,1)S(1)}, bf16[2,256,1024]{2,1,0:T(8,128)(2,1)S(1)}, f32[2,64,4096]{2,1,0...) custom-call(bf16[2,64,4096]{2,1,0:T(8,128)(2,1)S(1)} %get-tuple-elem, ...), custom_call_target="tpu_custom_call" | custom-call | tf_op jit(solution)/shard_map/update/pallas_call | solution.py:300
  178.1 163.3 %gather.1 = (bf16[2,2,2,2,2,64,4096]{6,5,4,3,2,1,0:T(8,128)(2,1)S(1)}, bf16[2,2,2,2,2,64,4096]{6,5,4,3,2,1,0:T(8,128)(2,1)S(1)}, bf16[2,2,2,2,2,256,1024]{6,5,4,3,2,1,0:T(8,128)(2,1)S(1)}) custom-call(bf16[2,64,4096]{2,1,0:T(8,128)(2,1)S(1)} %get-tuple-element.50.refs_0_, bf16[2,64,4096]{2,1,0:T(8,128)(2,1)S(1)} %get-tuple-element.51.refs_1_, ...), custom_call_target="tpu_custom_call" | custom-call | tf_op jit(solution)/shard_map/gather/pallas_call | solution.py:430
  341.3 16.1 %land.1 = (bf16[2,2,2,2,2,64,4096]{6,5,4,3,2,1,0:T(8,128)(2,1)}, bf16[2,2,2,2,2,64,4096]{6,5,4,3,2,1,0:T(8,128)(2,1)}, bf16[2,2,2,2,2,256,1024]{6,5,4,3,2,1,0:T(8,128)(2,1)}) custom-call(bf16[2,2,2,2,2,64,4096]{6,5,4,3,2,1,0:T(8,128)(2,1)S(1)} %get-tuple-element.53.refs_0_, bf16[2,2,2,2,2,64,4096]{6,5,4,3,2,1,0:T(8,128)(2,1)S(1)} %get-tuple-element.54.refs_1_, ...), custom_call_target="tpu_custom_call" | custom-call | tf_op jit(solution)/shard_map/land/pallas_call | solution.py:439
